TPU v7x, 128 devices: a whole 4x4x4 slice. The times are simulated.
128 devices in a mesh: section: 4 (over y_hi, core), fsdp: 32 (over y_lo, x, z).
Axes of the slice: x: 4, y: 4 (y_hi: 2, y_lo: 2; y = y_hi * 2 + y_lo), z: 4, core: 2. Of those that a mesh axis runs over, the one named last changes fastest.
Arguments:
- old_pieces: bfloat16 [4, 2, 16384, 1024], P('section', None, 'fsdp'), may hold values from -0.0625 to 0.0625
- section_inputs: bfloat16 [4, 16384, 8192], P('section', 'fsdp'), may hold values from -6 to 6
- old_section_of: int32 [8], replicated, may hold values from 0 to 3, as said below
- new_section_of: int32 [8], replicated, may hold values from 0 to 7, as said below
- old_order: int32 [8, 2], replicated, may hold values from 0 to 1, each once within a row
- new_order: int32 [8, 2], replicated, may hold values from 0 to 1, each once within a row
Outputs:
- new_shards: bfloat16 [4, 32768, 1024], P('section', 'fsdp')
- kv_out: bfloat16 [4, 16384, 2048], P('section', 'fsdp')
Inputs may be any that keep to these rules, and one draw needn't show every extreme that they name: `old_section_of`: each old section holds exactly two layers. Each new section holds exactly one layer; the two layers of one old section have different values of new_section_of // 2.
All inputs are finite; a program needn't handle non-finite values.
Results may differ from a plain program's by a relative error of at most 0.001.
Values may be sent and summed in bfloat16 or wider, within the bound.
A program may use at most 192 MiB of HBM per device.

v0:
```python
import math

import jax
import jax.numpy as jnp
from jax import lax
from jax.sharding import PartitionSpec as P

HEAD_DIM = 128


def from_partner(block, axis, stride):
    count = lax.axis_size(axis)
    route = []
    for low in range(count):
        high = low | 1 << stride
        if high != low and high < count:
            route += [(low, high), (high, low)]
    return lax.ppermute(block, axis, route)


def rotate_keys(values, positions):
    tok_rows = values.shape[0]
    heads = values.reshape(tok_rows, -1, HEAD_DIM)
    half_dim = HEAD_DIM // 2
    freq_index = jnp.arange(half_dim, dtype=jnp.float32)
    inverse_freq = jnp.exp(freq_index * (-2.0 * math.log(500000.0) / HEAD_DIM))
    angles = positions.astype(jnp.float32)[:, None] * inverse_freq[None, :]
    cosine = jnp.cos(angles)[:, None, :]
    sine = jnp.sin(angles)[:, None, :]
    lower = heads[..., :half_dim]
    upper = heads[..., half_dim:]
    turned = jnp.concatenate(
        [lower * cosine - upper * sine, upper * cosine + lower * sine], axis=-1
    )
    return turned.reshape(tok_rows, -1)


def pick_entry(table, index_value):
    positions = jnp.arange(table.shape[0], dtype=jnp.int32)
    return jnp.sum(jnp.where(positions == index_value, table, 0))


def pick_row(table, index_value):
    positions = jnp.arange(table.shape[0], dtype=jnp.int32)[:, None]
    return jnp.sum(jnp.where(positions == index_value, table, 0), axis=0)


def per_device(old_pieces, section_inputs, old_section_of, new_section_of, old_order, new_order):
    section_count = lax.axis_size("section")
    member_count = lax.axis_size("fsdp")
    digit_count = member_count.bit_length() - 1
    row_index = lax.axis_index("section")
    member = lax.axis_index("fsdp")
    parity = member % 2
    layer_total = old_section_of.shape[0]
    layer_ids = jnp.arange(layer_total, dtype=jnp.int32)
    in_row = old_section_of == row_index
    layer_low = jnp.min(jnp.where(in_row, layer_ids, layer_total))
    layer_high = jnp.max(jnp.where(in_row, layer_ids, -1))
    target_low = pick_entry(new_section_of, layer_low) // 2
    target_high = pick_entry(new_section_of, layer_high) // 2
    pieces = old_pieces[0]
    targets = jnp.arange(section_count, dtype=jnp.int32)[:, None, None]
    nothing = jnp.zeros_like(pieces[0])
    outgoing = jnp.where(
        targets == target_low,
        pieces[0][None],
        jnp.where(targets == target_high, pieces[1][None], nothing[None]),
    )
    incoming = lax.all_to_all(outgoing, "section", split_axis=0, concat_axis=0, tiled=True)
    layer_own = jnp.sum(jnp.where(new_section_of == 2 * row_index + parity, layer_ids, 0))
    layer_foreign = jnp.sum(jnp.where(new_section_of == 2 * row_index + 1 - parity, layer_ids, 0))
    own_piece = lax.dynamic_index_in_dim(
        incoming, pick_entry(old_section_of, layer_own), 0, keepdims=False
    )
    foreign_piece = lax.dynamic_index_in_dim(
        incoming, pick_entry(old_section_of, layer_foreign), 0, keepdims=False
    )
    partner_piece = from_partner(foreign_piece, "fsdp", 0)
    lower = jnp.where(parity == 0, own_piece, partner_piece)
    upper = jnp.where(parity == 0, partner_piece, own_piece)
    holding = jnp.concatenate([lower, upper], axis=0)
    tokens = section_inputs[0]
    tok_rows, model_width = tokens.shape
    shard_rows, kv_width = holding.shape
    own_bits = {digit: member // 2**digit % 2 for digit in range(1, digit_count)}
    own_old = pick_row(old_order, layer_own)
    own_new = pick_row(new_order, layer_own)
    flipped = own_old[0] != own_new[0]
    group_digits = digit_count - 1
    low_count = group_digits // 2
    high_digits = list(range(low_count + 1, digit_count))
    low_digits = list(range(1, low_count + 1))
    gathered = holding
    digits_done = []
    for digit in high_digits:
        received = from_partner(gathered, "fsdp", digit)
        bit_value = own_bits[digit]
        lower = jnp.where(bit_value == 0, gathered, received)
        upper = jnp.where(bit_value == 0, received, gathered)
        position = len([other_digit for other_digit in digits_done if other_digit > digit])
        gathered = jnp.stack([lower, upper], axis=position)
        digits_done = sorted(digits_done + [digit], reverse=True)
    block_count = gathered.shape[1]
    column_view = tokens.reshape((tok_rows, block_count) + (2,) * low_count + (shard_rows,))
    for digit in low_digits:
        axis_index = 2 + (low_count - digit)
        bit_value = own_bits[digit]
        mine = lax.dynamic_index_in_dim(column_view, bit_value, axis_index, keepdims=False)
        other = lax.dynamic_index_in_dim(column_view, 1 - bit_value, axis_index, keepdims=False)
        received = from_partner(other, "fsdp", digit)
        lower = jnp.where(bit_value == 0, mine, received)
        upper = jnp.where(bit_value == 0, received, mine)
        column_view = jnp.stack([lower, upper], axis=axis_index)
    token_blocks = column_view.reshape(tok_rows, block_count, 2**low_count, shard_rows)
    partial_value = jnp.einsum(
        "tabi,saik->sbtk", token_blocks, gathered, preferred_element_type=jnp.float32
    )
    partial_value = partial_value.reshape((2,) + (2,) * low_count + (tok_rows, kv_width))
    for digit in low_digits:
        axis_index = 1 + (low_count - digit)
        bit_value = own_bits[digit]
        mine = lax.dynamic_index_in_dim(partial_value, bit_value, axis_index, keepdims=True)
        other = lax.dynamic_index_in_dim(partial_value, 1 - bit_value, axis_index, keepdims=True)
        received = from_partner(other, "fsdp", digit)
        partial_value = mine + received
    totals = partial_value.reshape(2, tok_rows, kv_width)
    top_bit = own_bits[digit_count - 1]
    matrix_index = jnp.where(flipped, 1 - top_bit, top_bit)
    block_index = member // 2 // 2**low_count % block_count
    chosen_matrix = lax.dynamic_index_in_dim(gathered, matrix_index, 0, keepdims=False)
    new_shard = lax.dynamic_index_in_dim(chosen_matrix, block_index, 0, keepdims=False)
    keys = jnp.where(own_old[0] == 0, totals[0], totals[1])
    values = jnp.where(own_old[1] == 0, totals[0], totals[1])
    positions = member // 2 * tok_rows + jnp.arange(tok_rows, dtype=jnp.int32)
    joined = jnp.concatenate([rotate_keys(keys, positions), values], axis=-1).astype(jnp.bfloat16)
    return (new_shard[None], joined[None])


def solution(mesh):
    in_specs = (P("section", None, "fsdp", None), P("section", "fsdp", None), P(), P(), P(), P())
    out_specs = (P("section", "fsdp", None), P("section", "fsdp", None))
    return jax.shard_map(
        per_device, mesh=mesh, in_specs=in_specs, out_specs=out_specs, check_vma=False
    )
```

profile of v0, /device:TPU:1, one launch (start us, length us, event | category | flops | bytes accessed | tf_op | source)
XLA Modules:
  0.0 663.1 jit_solution(13618215659930264838)
XLA Ops:
  17.5 6.3 all-to-all-start
  23.8 12.0 %copy.21 = bf16[1,512,8192]{1,2,0:T(8,128)(2,1)} copy(bf16[1,512,8192]{2,1,0:T(8,128)(2,1)} %param.7) | data formatting | bytes 16777216 | tf_op args[1]
  35.8 7.2 %constant_dynamic-slice_fusion.4 = (bf16[512,2,2,1,1024]{0,4,3,2,1:T(8,128)(2,1)}, bf16[512,2,2,1,1024]{0,4,3,2,1:T(8,128)(2,1)}) fusion(bf16[512,2,2,2,1024]{0,4,3,2,1:T(8,128)(2,1)} %bitcast.69, s32[]{:T(128)S(6)} %select_n.260, s32[]{:T(128)S(6)} %select_n.261), kind=kLoop, calls=%fused_computation.47 | loop fusion | bytes 16777224 | tf_op jit(solution)/shard_map/jit(dynamic_index_in_dim)/dynamic_slice | solution.py:109
  43.0 6.3 copy.23
  49.3 3.7 collective-permute-start.3
  55.0 17.6 %all-to-all-done = bf16[4,512,1024]{1,2,0:T(8,128)(2,1)} async-done(((bf16[4,512,1024]{1,2,0:T(8,128)(2,1)}), bf16[4,512,1024]{1,2,0:T(8,128)(2,1)}, u32[]{:S(2)}, u32[]{:S(2)}) %all-to-all-start) | async-done | bytes 4194336 | tf_op jit(solution)/shard_map/all_to_all | solution.py:70
  77.4 89.6 %collective-permute-done = bf16[512,1024]{0,1:T(8,128)(2,1)S(1)} collective-permute-done((bf16[512,1024]{0,1:T(8,128)(2,1)S(1)}, bf16[512,1024]{0,1:T(8,128)(2,1)S(1)}, u32[]{:S(2)}, u32[]{:S(2)}) %collective-permute-start) | collective-permute-done | bytes 1048608 | tf_op jit(solution)/shard_map/ppermute | solution.py:18
  172.4 6.4 copy.22
  178.8 3.8 fusion.8
  187.4 30.2 %collective-permute-done.1 = bf16[1024,1024]{0,1:T(8,128)(2,1)} collective-permute-done((bf16[1024,1024]{0,1:T(8,128)(2,1)S(1)}, bf16[1024,1024]{0,1:T(8,128)(2,1)}, u32[]{:S(2)}, u32[]{:S(2)}) %collective-permute-start.1) | collective-permute-done | bytes 2097184 | tf_op jit(solution)/shard_map/ppermute | solution.py:18
  217.5 2.8 select_bitcast_fusion.6
  224.4 83.1 %collective-permute-done.4 = bf16[512,2,2,1024]{3,0,1,2:T(8,128)(2,1)} collective-permute-done((bf16[512,2,2,1024]{3,0,1,2:T(8,128)(2,1)}, bf16[512,2,2,1024]{3,0,1,2:T(8,128)(2,1)}, u32[]{:S(2)}, u32[]{:S(2)}) %collective-permute-start.4) | collective-permute-done | bytes 4194336 | tf_op jit(solution)/shard_map/ppermute | solution.py:18
  307.5 8.3 %select_bitcast_fusion.1 = (bf16[512,2,1,2,1024]{4,0,1,3,2:T(8,128)(2,1)}, bf16[512,2,1,2,1024]{4,0,1,3,2:T(8,128)(2,1)}) fusion(bf16[512,2,2,1024]{3,0,1,2:T(8,128)(2,1)} %collective-permute-done.4, pred[]{:T(512)S(6)} %eq.135, s32[]{:T(128)S(6)} %select_n.264, bf16[512,2,2,1,1024]{4,0,2,1,3:T(8,128)(2,1)} %copy-done, bf16[512,2,2,1,1024]{4,0,2,1,3:T(8,128)(2,1)} %copy-done.1), kind=kLoop, calls=%fused_computation.21 | loop fusion | flops 8388608 | bytes 20971524 | tf_op jit(solution)/shard_map/stack | solution.py:114
  315.8 7.6 %pad_maximum_fusion.1 = bf16[512,2,2,2,1024]{4,0,1,3,2:T(8,128)(2,1)} fusion(bf16[512,2,1,2,1024]{4,0,1,3,2:T(8,128)(2,1)} %get-tuple-element.15, bf16[512,2,1,2,1024]{4,0,1,3,2:T(8,128)(2,1)} %get-tuple-element.14), kind=kLoop, calls=%fused_computation.9 | loop fusion | flops 4194304 | bytes 16777216 | tf_op jit(solution)/shard_map/stack | solution.py:114
  323.4 5.1 select_bitcast_fusion.2
  328.5 21.7 %fusion.1 = f32[2,1024,512,4,1]{2,1,4,3,0:T(8,128)S(1)} fusion(bf16[512,2,4,1024,1]{3,0,1,2,4:T(8,128)(2,1)} %bitcast.72, bf16[1,2,1024,1024]{2,3,1,0:T(8,128)(2,1)} %get-tuple-element.20, bf16[1,2,1024,1024]{2,3,1,0:T(8,128)(2,1)} %get-tuple-element.21), kind=kOutput, calls=%fused_computation.8 | convolution fusion | flops 17196646400 | bytes 33554432 | tf_op jit(solution)/shard_map/tabi,saik->sbtk/dot_general | solution.py:116
  350.2 6.7 %constant_dynamic-slice_fusion.1 = (f32[2,2,1,512,1024]{3,4,2,1,0:T(8,128)}, f32[2,2,1,512,1024]{3,4,2,1,0:T(8,128)}) fusion(f32[2,2,2,512,1024]{3,4,2,1,0:T(8,128)S(1)} %bitcast.71, s32[]{:T(128)S(6)} %select_n.261, s32[]{:T(128)S(6)} %select_n.260), kind=kLoop, calls=%fused_computation.44 | loop fusion | bytes 33554440 | tf_op jit(solution)/shard_map/jit(dynamic_index_in_dim)/dynamic_slice | solution.py:124
  356.9 8.7 %copy.29 = f32[2,2,1,512,1024]{4,3,2,1,0:T(8,128)} copy(f32[2,2,1,512,1024]{3,4,2,1,0:T(8,128)} %get-tuple-element.12) | data formatting | bytes 16777216
  366.5 8.7 %copy.28 = f32[2,2,1,512,1024]{4,3,2,1,0:T(8,128)} copy(f32[2,2,1,512,1024]{3,4,2,1,0:T(8,128)} %get-tuple-element.13) | data formatting | bytes 16777216
  375.3 172.4 %collective-permute-done.5 = f32[2,2,1,512,1024]{4,3,2,1,0:T(8,128)} collective-permute-done((f32[2,2,1,512,1024]{4,3,2,1,0:T(8,128)}, f32[2,2,1,512,1024]{4,3,2,1,0:T(8,128)}, u32[]{:S(2)}, u32[]{:S(2)}) %collective-permute-start.5) | collective-permute-done | bytes 8388640 | tf_op jit(solution)/shard_map/ppermute | solution.py:18
  547.7 12.0 %add.108 = f32[2,2,1,512,1024]{4,3,2,1,0:T(8,128)} add(f32[2,2,1,512,1024]{4,3,2,1,0:T(8,128)} %copy.28, f32[2,2,1,512,1024]{4,3,2,1,0:T(8,128)} %collective-permute-done.5) | non-fusion elementwise | flops 2097152 | bytes 25165824 | tf_op jit(solution)/shard_map/add | solution.py:126
  559.6 4.8 constant_dynamic-slice_fusion
  574.8 79.4 %collective-permute-done.6 = f32[2,1,1,512,1024]{4,3,2,1,0:T(8,128)} collective-permute-done((f32[2,1,1,512,1024]{4,3,2,1,0:T(8,128)}, f32[2,1,1,512,1024]{4,3,2,1,0:T(8,128)}, u32[]{:S(2)}, u32[]{:S(2)}) %collective-permute-start.6) | collective-permute-done | bytes 4194336 | tf_op jit(solution)/shard_map/ppermute | solution.py:18
  654.2 4.4 dynamic-slice_add_fusion
  (50 shorter events, 42.8 us)
Async XLA Ops:
  17.5 55.0 %all-to-all-start = ((bf16[4,512,1024]{1,2,0:T(8,128)(2,1)}), bf16[4,512,1024]{1,2,0:T(8,128)(2,1)}, u32[]{:S(2)}, u32[]{:S(2)}) async-start(bf16[4,512,1024]{1,2,0:T(8,128)(2,1)} %select_select_fusion), calls=%async_computation | async-start | bytes 8388608 | tf_op jit(solution)/shard_map/all_to_all | solution.py:70
  49.3 129.5 %collective-permute-start.3 = (bf16[512,2,2,1024]{3,0,2,1:T(8,128)(2,1)}, bf16[512,2,2,1024]{3,0,2,1:T(8,128)(2,1)}, u32[]{:S(2)}, u32[]{:S(2)}) collective-permute-start(bf16[512,2,2,1024]{3,0,2,1:T(8,128)(2,1)} %bitcast.73), channel_id=1, source_target_pairs={{0,2},{2,0},{1,3},{3,1},{4,6},{6,4},{5,7},{7,5},{8,10},{10,8},{9,1... | collective-permute-start | bytes 12582920 | tf_op jit(solution)/shard_map/ppermute | solution.py:18
  73.9 93.1 %collective-permute-start = (bf16[512,1024]{0,1:T(8,128)(2,1)S(1)}, bf16[512,1024]{0,1:T(8,128)(2,1)S(1)}, u32[]{:S(2)}, u32[]{:S(2)}) collective-permute-start(bf16[512,1024]{0,1:T(8,128)(2,1)S(1)} %dynamic-slice_bitcast_fusion), channel_id=1, source_target_pairs={{0,1},{1,0},{2,3},{3,2},{4,5},{5,4},{6,7},{7,6},{8,9},{9,8},{10,11... | collective-permute-start | bytes 3145736 | tf_op jit(solution)/shard_map/ppermute | solution.py:18
  168.3 1.0 copy-start.4
  169.6 47.9 %collective-permute-start.1 = (bf16[1024,1024]{0,1:T(8,128)(2,1)S(1)}, bf16[1024,1024]{0,1:T(8,128)(2,1)}, u32[]{:S(2)}, u32[]{:S(2)}) collective-permute-start(bf16[1024,1024]{0,1:T(8,128)(2,1)S(1)} %pad_maximum_fusion.3), channel_id=1, source_target_pairs={{0,8},{8,0},{1,9},{9,1},{2,10},{10,2},{3,11},{11,3},{4,12},{12,4},... | collective-permute-start | bytes 6291464 | tf_op jit(solution)/shard_map/ppermute | solution.py:18
  182.6 3.2 copy-start
  182.6 4.5 copy-start.1
  187.0 120.5 %collective-permute-start.4 = (bf16[512,2,2,1024]{3,0,1,2:T(8,128)(2,1)}, bf16[512,2,2,1024]{3,0,1,2:T(8,128)(2,1)}, u32[]{:S(2)}, u32[]{:S(2)}) collective-permute-start(bf16[512,2,2,1024]{3,0,1,2:T(8,128)(2,1)} %fusion.4), channel_id=1, source_target_pairs={{0,4},{4,0},{1,5},{5,1},{2,6},{6,2},{3,7},{7,3},{8,12},{12,8},{9,1... | collective-permute-start | bytes 12582920 | tf_op jit(solution)/shard_map/ppermute | solution.py:18
  220.4 2.7 copy-start.2
  223.1 100.3 %collective-permute-start.2 = (bf16[2,1024,1024]{1,2,0:T(8,128)(2,1)}, bf16[2,1024,1024]{1,2,0:T(8,128)(2,1)}, u32[]{:S(2)}, u32[]{:S(2)}) collective-permute-start(bf16[2,1024,1024]{1,2,0:T(8,128)(2,1)} %pad_maximum_fusion.2), channel_id=1, source_target_pairs={{0,16},{16,0},{1,17},{17,1},{2,18},{18,2},{3,19},{19,3},{4,20},{20... | collective-permute-start | bytes 12582920 | tf_op jit(solution)/shard_map/ppermute | solution.py:18
  315.8 7.6 %copy-start.3 = (bf16[1,1024,1024]{1,2,0:T(8,128)(2,1)S(1)}, bf16[1,1024,1024]{1,2,0:T(8,128)(2,1)}, u32[]{:S(2)}) copy-start(bf16[1,1024,1024]{1,2,0:T(8,128)(2,1)} %copy-done.2) | copy-start | bytes 6291460
  365.7 182.0 %collective-permute-start.5 = (f32[2,2,1,512,1024]{4,3,2,1,0:T(8,128)}, f32[2,2,1,512,1024]{4,3,2,1,0:T(8,128)}, u32[]{:S(2)}, u32[]{:S(2)}) collective-permute-start(f32[2,2,1,512,1024]{4,3,2,1,0:T(8,128)} %copy.29), channel_id=1, source_target_pairs={{0,2},{2,0},{1,3},{3,1},{4,6},{6,4},{5,7},{7,5},{8,10},{10,8},{9,1... | collective-permute-start | bytes 25165832 | tf_op jit(solution)/shard_map/ppermute | solution.py:18
  559.6 6.4 copy-start.5
  559.6 6.4 copy-start.6
  564.4 89.8 %collective-permute-start.6 = (f32[2,1,1,512,1024]{4,3,2,1,0:T(8,128)}, f32[2,1,1,512,1024]{4,3,2,1,0:T(8,128)}, u32[]{:S(2)}, u32[]{:S(2)}) collective-permute-start(f32[2,1,1,512,1024]{4,3,2,1,0:T(8,128)} %constant_dynamic-slice_fusion), channel_id=1, source_target_pairs={{0,4},{4,0},{1,5},{5,1},{2,6},{6,2},{3,7},{7,3},{8,12},{12,8},{9,1... | collective-permute-start | bytes 12582920 | tf_op jit(solution)/shard_map/ppermute | solution.py:18
where the time goes:
time: 667 us; the launch traced here: 663 us
  waiting for transfers between devices  472 us (71%)
  local copies, waits for them, and re-layouts  72 us (11%)
  other arithmetic  67.3 us (10%)
  matrix products  21.7 us (3%)
  starting transfers between devices  18.1 us (3%)
  between operations  11.7 us (2%)
    ppermute x7, waiting for transfers between devices, from_partner(): return lax.ppermute(block, axis, route)  455 us
    unnamed x18, local copies, waits for them, and re-layouts  32.9 us
    dot_general x1, matrix products, per_device(): jnp.einsum('tabi,saik->sbtk', token_blocks, gathered, preferred_element_t...  21.7 us
    another operation x3, other arithmetic, per_device(): column_view = jnp.stack([lower, upper], axis=axis_index)  19.6 us
    all_to_all x1, waiting for transfers between devices, per_device(): lax.all_to_all(outgoing, 'section', split_axis=0, concat_axis=0, tiled=True)  17.6 us
    add x2, other arithmetic, per_device(): partial_value = mine + received  16.4 us
    dynamic_slice x2, local copies, waits for them, and re-layouts, per_device(): lax.dynamic_index_in_dim(column_view, bit_value, axis_index, keepdims=False)  13.6 us
  transfers between devices with their start and end apart: 8, of which 6 were waited for; matrix products, arithmetic and copies ran while one was open for 12% of the time, Pallas kernels for 0%

commit v1 on v0

v1 whole, which is shorter than its diff:
```python
import math

import jax
import jax.numpy as jnp
from jax import lax
from jax.experimental import pallas as pl
from jax.experimental.pallas import tpu as pltpu
from jax.sharding import PartitionSpec as P

HEAD_DIM = 128
MESH = pl.DeviceIdType.MESH
NC = 8
NG = 4
TU = 8


def body(oldsec, newsec, oldord, neword, pieces, tokens, cos_in, sin_in, kv_out, shard_out,
         pc, og, cand, tb, sf, wb, n2, sha, shb, xb, acc, ob, ct, st,
         pc_sem, rs, rr, ws, wr, zs, zr, xs, xr, ns, nr, shl, shs, shr,
         tl, tas, tar, ts, tr, tfs, tfr, osm, orm, olm, tab_sem):
    rows = pieces.shape[1]
    cw = pieces.shape[2] // NC
    gw = pieces.shape[2] // NG
    per = NC // NG
    tok_rows, width = tokens.shape
    layers = oldsec.shape[0]
    s = lax.axis_index("section")
    m = lax.axis_index("fsdp")
    y = s // 2
    c = s % 2
    j = m // 16
    x = (m // 4) % 4
    z = m % 4
    h = z % 2
    is_a = c == j
    is_b = c != j

    def dev(yy, cc, jj, xx, zz):
        return (2 * yy + cc, jj * 16 + xx * 4 + zz)

    core_dev = dev(y, 1 - c, j, x, z)
    cross_dev = [dev(1 - y, k, 1 - j, x, z) for k in range(2)]
    side_dev = [dev(y, k, 1 - j, x, z) for k in range(2)]
    zp, zm, zf = (z + 1) % 4, (z + 3) % 4, (z + 2) % 4
    xp, xm, xf = (x + 1) % 4, (x + 3) % 4, (x + 2) % 4
    zp_dev, zm_dev, zf_dev = (dev(y, c, j, x, zz) for zz in (zp, zm, zf))
    xp_dev, xm_dev = (dev(y, c, j, xx, z) for xx in (xp, xm))

    def remote(src, dst, send, recv, device):
        return pltpu.make_async_remote_copy(
            src_ref=src, dst_ref=dst, send_sem=send, recv_sem=recv,
            device_id=device, device_id_type=MESH)

    def arrived(dst, send, recv, device):
        remote(dst, dst, send, recv, device).wait_recv()

    def pc_copy(i, a):
        return pltpu.make_async_copy(
            pieces.at[a, :, pl.ds(i * cw, cw)], pc.at[i, a], pc_sem.at[i, a])

    for i in range(NC):
        for a in range(2):
            pc_copy(i, a).start()
    table_copies = [pltpu.make_async_copy(cos_in, ct, tab_sem.at[0]),
                    pltpu.make_async_copy(sin_in, st, tab_sem.at[1])]
    for copy in table_copies:
        copy.start()

    def layer_of(section):
        found = jnp.int32(0)
        for l in range(layers):
            found = found + jnp.where(newsec[l] == section, l, 0)
        return found

    def entry(table, layer):
        found = jnp.int32(0)
        for l in range(layers):
            found = found + jnp.where(layer == l, table(l), 0)
        return found

    high = jnp.int32(0)
    for l in range(layers):
        high = jnp.where(oldsec[l] == s, l, high)
    row_high = entry(lambda l: newsec[l], high) // 2
    source = [entry(lambda l: oldsec[l], layer_of(2 * s + k)) for k in range(2)]
    source_own = jnp.where(h == 0, source[0], source[1])
    source_other = jnp.where(h == 0, source[1], source[0])
    gl = layer_of(2 * (2 * y + j) + h)
    gl_crossed = jnp.where(entry(lambda l: oldsec[l], gl) // 2 == y, 0, 1)
    gl_old = entry(lambda l: oldord[2 * l], gl)
    gl_new = entry(lambda l: neword[2 * l], gl)
    gl_turn = (jnp.where(gl_old == gl_new, 0, 1) + gl_crossed) % 2
    is_key = gl_old == (c + gl_crossed) % 2

    barrier = pltpu.get_barrier_semaphore()
    partners = [core_dev] + cross_dev + side_dev + [zp_dev, zm_dev, zf_dev, xp_dev, xm_dev]
    for device in partners:
        pl.semaphore_signal(barrier, inc=1, device_id=device, device_id_type=MESH)
    pl.semaphore_wait(barrier, len(partners))

    tok_step = width // (2 * TU)
    quarter = width // 4

    def tok_send(v):
        u, a = v // 2, v % 2
        cols = pl.ds((a * TU + u) * tok_step, tok_step)
        return remote(tokens.at[:, cols], xb.at[1, :, cols], ts.at[v], tr.at[u], side_dev[a])

    def tok_here(u):
        cols = pl.ds(pl.multiple_of((c * TU + u) * tok_step, 128), tok_step)
        return remote(xb.at[1, :, cols], xb.at[1, :, cols], tfs.at[u], tr.at[u], core_dev)

    def tok_pass(u):
        cols = pl.ds(pl.multiple_of((c * TU + u) * tok_step, 128), tok_step)
        return remote(xb.at[1, :, cols], xb.at[1, :, cols], tfs.at[u], tfr.at[u], core_dev)

    def tok_other(u):
        cols = pl.ds(pl.multiple_of(((1 - c) * TU + u) * tok_step, 128), tok_step)
        return remote(xb.at[1, :, cols], xb.at[1, :, cols], tfs.at[u], tfr.at[u], core_dev)

    def tok_core(k):
        cols = pl.ds(k * quarter, quarter)
        return remote(tokens.at[:, cols], xb.at[0, :, cols], tas.at[k], tar.at[k], core_dev)

    tok_local = pltpu.make_async_copy(tokens, xb.at[0], tl.at[0])
    tok_next = [0]

    def send_tokens(count):
        take = range(tok_next[0], min(tok_next[0] + count, 2 * TU))
        tok_next[0] += len(take)

        @pl.when(is_b)
        def _():
            for v in take:
                tok_send(v).start()

    def relay_copies(i):
        return [remote(og.at[i, k], cand.at[i, s], rs.at[i, k],
                       rr.at[i, 0] if k == 0 else rr.at[i, 1 + c], device)
                for k, device in enumerate([core_dev] + cross_dev)]

    relay_rows = [2 * y + 1 - c, 2 * (1 - y), 2 * (1 - y) + 1]

    def relay_send(i):
        for a in range(2):
            pc_copy(i, a).wait()

        def tile(t, carry):
            part = pl.ds(pl.multiple_of(t * 128, 128), 128)
            low_rows = pc[i, 0, part, :]
            high_rows = pc[i, 1, part, :]
            for k in range(3):
                og[i, k, part, :] = jnp.where(row_high == relay_rows[k], high_rows, low_rows)
            cand[i, s, part, :] = jnp.where(row_high == s, high_rows, low_rows)
            return carry

        lax.fori_loop(0, rows // 128, tile, 0)
        for copy in relay_copies(i):
            copy.start()

    place = pl.ds(pl.multiple_of((x * 4 + z) * rows, rows), rows)

    def swap_copies(i):
        device = dev(y, 1 - c, 1 - j, x, z)
        return [remote(tb.at[i, 0], wb.at[i, place], ws.at[i, 0], wr.at[i, 0], device),
                remote(tb.at[i, 1], sf.at[i], ws.at[i, 1], wr.at[i, 1], device)]

    def choose(i):
        arrived(cand.at[i, 2 * y + 1 - c], rs.at[i, 0], rr.at[i, 0], core_dev)
        for k in range(2):
            arrived(cand.at[i, 2 * (1 - y) + k], rs.at[i, 1 + k], rr.at[i, 1 + k], cross_dev[k])

        def picked(part):
            four = [cand[i, k, part, :] for k in range(4)]
            out = []
            for want in (source_own, source_other):
                out.append(jnp.where(want < 2, jnp.where(want == 0, four[0], four[1]),
                                     jnp.where(want == 2, four[2], four[3])))
            return out

        @pl.when(is_a)
        def _():
            def tile(t, carry):
                part = pl.ds(pl.multiple_of(t * 128, 128), 128)
                mine, other = picked(part)
                wb[i, pl.ds(pl.multiple_of((x * 4 + z) * rows + t * 128, 128), 128), :] = mine
                sf[i, part, :] = other
                return carry

            lax.fori_loop(0, rows // 128, tile, 0)

        @pl.when(is_b)
        def _():
            def tile(t, carry):
                part = pl.ds(pl.multiple_of(t * 128, 128), 128)
                mine, other = picked(part)
                tb[i, 0, part, :] = mine
                tb[i, 1, part, :] = other
                return carry

            lax.fori_loop(0, rows // 128, tile, 0)
            for copy in swap_copies(i):
                copy.start()

    def z_copies(i):
        return [remote(sf.at[i], wb.at[i, place], zs.at[i, 0], zr.at[i, 0], zp_dev),
                remote(sf.at[i], wb.at[i, place], zs.at[i, 1], zr.at[i, 1], zm_dev),
                remote(wb.at[i, place], wb.at[i, place], zs.at[i, 2], zr.at[i, 2], zf_dev)]

    def z_send(i):
        @pl.when(is_b)
        def _():
            for copy in swap_copies(i):
                copy.wait_recv()
        for copy in z_copies(i):
            copy.start()

    def block(i, xx, first, count):
        return wb.at[i, pl.ds(pl.multiple_of(xx * 4 * rows + first, rows), count)]

    def own_copies(i):
        mine = block(i, x, 0, 4 * rows)
        return [remote(mine, mine, xs.at[i, 0], xr.at[i, 0], xp_dev),
                remote(mine, mine, xs.at[i, 1], xr.at[i, 1], xm_dev)]

    def pass_copies(i):
        left = block(i, xm, 0, 2 * rows)
        right = block(i, xp, 2 * rows, 2 * rows)
        return [remote(left, left, xs.at[i, 2], xr.at[i, 2], xp_dev),
                remote(right, right, xs.at[i, 3], xr.at[i, 3], xm_dev)]

    pair = pl.ds(pl.multiple_of((x * 4 + z // 2 * 2) * rows, rows), 2 * rows)

    def near_copy(i):
        return remote(wb.at[i, pair], n2.at[i], ns.at[i], nr.at[i], core_dev)

    def x_own(i):
        for k, zz in enumerate((zm, zp, zf)):
            arrived(block(i, x, zz * rows, rows), zs.at[i, k], zr.at[i, k], zf_dev)
        for copy in own_copies(i):
            copy.start()

        @pl.when(is_b)
        def _():
            near_copy(i).start()

    def x_pass(i):
        arrived(block(i, xm, 0, 4 * rows), xs.at[i, 0], xr.at[i, 0], xp_dev)
        first, second = pass_copies(i)
        first.start()
        arrived(block(i, xp, 0, 4 * rows), xs.at[i, 1], xr.at[i, 1], xm_dev)
        second.start()

    def far_arrived(i):
        arrived(block(i, xf, 0, 2 * rows), xs.at[i, 2], xr.at[i, 2], xp_dev)
        arrived(block(i, xf, 2 * rows, 2 * rows), xs.at[i, 3], xr.at[i, 3], xm_dev)

    def shard_local(i):
        return pltpu.make_async_copy(sha.at[i], shard_out.at[:, pl.ds(i * cw, cw)], shl.at[i])

    def shard_far(i):
        return remote(shb.at[i], shard_out.at[:, pl.ds(i * cw, cw)], shs.at[i], shr.at[i],
                      dev(y, c, 1 - j, x, z))

    def shard(i):
        @pl.when(is_a)
        def _():
            near_copy(i).wait_recv()

            def tile(t, carry):
                part = pl.ds(pl.multiple_of(t * 128, 128), 128)
                near = pl.ds(pl.multiple_of((x * 4 + z // 2 * 2) * rows + t * 128, 128), 128)
                mine = wb[i, near, :]
                other = n2[i, part, :]
                sha[i, part, :] = jnp.where(gl_turn == 0, mine, other)
                shb[i, part, :] = jnp.where(gl_turn == 0, other, mine)
                return carry

            lax.fori_loop(0, 2 * rows // 128, tile, 0)

    def shard_send(i):
        @pl.when(is_a)
        def _():
            shard_local(i).start()
            shard_far(i).start()

    def multiply(g, xx, half):
        first = pl.multiple_of(xx * 4 * rows + half * 2 * rows, 2 * rows)
        ks = pl.ds(first, 2 * rows)
        weight = jnp.concatenate([wb[per * g + k, ks, :] for k in range(per)], axis=1)
        for slot in range(2):
            acc[slot] += jnp.dot(xb[slot, :, ks], weight, preferred_element_type=jnp.float32)

    def finish(g):
        def tile(t, carry):
            part = pl.ds(pl.multiple_of(t * 64, 64), 64)
            for slot in range(2):
                cosine = ct[slot, part, :]
                sine = st[slot, part, :]
                for head in range(gw // HEAD_DIM):
                    cols = slice(head * HEAD_DIM, (head + 1) * HEAD_DIM)
                    value = acc[slot, part, cols]
                    turned = value * cosine + pltpu.roll(value, HEAD_DIM // 2, 1) * sine
                    ob[g, slot, part, cols] = turned.astype(jnp.bfloat16)
            return carry

        lax.fori_loop(0, tok_rows // 64, tile, 0)

    def out_local(g):
        return pltpu.make_async_copy(
            ob.at[g, 0], kv_out.at[c, :, pl.ds(g * gw, gw)], olm.at[g])

    def out_near(g):
        return remote(ob.at[g, 0], kv_out.at[c, :, pl.ds(g * gw, gw)],
                      osm.at[g, 0], orm.at[g, c], core_dev)

    def out_far(g):
        return remote(ob.at[g, 1], kv_out.at[c, :, pl.ds(g * gw, gw)],
                      osm.at[g, 1], orm.at[g, c], dev(y, j, 1 - j, x, z))

    def out_send(g):
        out_far(g).start()

        @pl.when(is_a)
        def _():
            out_local(g).start()

        @pl.when(is_b)
        def _():
            out_near(g).start()

    send_tokens(1)
    for i in range(NC):
        relay_send(i)

    @pl.when(is_a)
    def _():
        tok_local.start()
        for k in range(4):
            tok_core(k).start()

    for copy in table_copies:
        copy.wait()

    def table_tile(t, carry):
        part = pl.ds(pl.multiple_of(t * 64, 64), 64)
        for slot in range(2):
            ct[slot, part, :] = jnp.where(is_key, ct[slot, part, :], 1.0)
            st[slot, part, :] = jnp.where(is_key, st[slot, part, :], 0.0)
        return carry

    lax.fori_loop(0, tok_rows // 64, table_tile, 0)

    choose(0)
    send_tokens(1)
    for i in range(NC):
        z_send(i)
        if i + 1 < NC:
            choose(i + 1)
            send_tokens(1)
        x_own(i)
    send_tokens(2 * TU)
    for i in range(NC):
        x_pass(i)
        shard(i)
        if i < TU:
            tok_here(i).wait_recv()
            tok_pass(i).start()
    for i in range(NC):
        shard_send(i)

    @pl.when(is_a)
    def _():
        tok_local.wait()

    @pl.when(is_b)
    def _():
        for k in range(4):
            tok_core(k).wait_recv()

    for u in range(TU):
        tok_other(u).wait_recv()

    for g in range(NG):
        acc[...] = jnp.zeros_like(acc)

        def near_block(t, carry):
            b = t // 2
            multiply(g, (x + b + b // 2) % 4, t % 2)
            return carry

        lax.fori_loop(0, 6, near_block, 0)
        for k in range(per):
            far_arrived(per * g + k)

        def far_block(t, carry):
            multiply(g, xf, t)
            return carry

        lax.fori_loop(0, 2, far_block, 0)
        finish(g)
        out_send(g)

    for i in range(NC):
        for copy in relay_copies(i) + z_copies(i) + own_copies(i) + pass_copies(i):
            copy.wait_send()

    @pl.when(is_a)
    def _():
        for k in range(4):
            tok_core(k).wait_send()
        for i in range(NC):
            shard_local(i).wait()
            shard_far(i).wait_send()
        for g in range(NG):
            out_local(g).wait()
            arrived(kv_out.at[1 - c, :, pl.ds(g * gw, gw)], osm.at[g, 0], orm.at[g, 1 - c], core_dev)

    @pl.when(is_b)
    def _():
        for v in range(2 * TU):
            tok_send(v).wait_send()
        for i in range(NC):
            for copy in swap_copies(i):
                copy.wait_send()
            near_copy(i).wait_send()
            shard_far(i).wait_recv()
        for g in range(NG):
            out_near(g).wait_send()
            for k in range(2):
                arrived(kv_out.at[k, :, pl.ds(g * gw, gw)], osm.at[g, 0], orm.at[g, k], side_dev[k])

    for u in range(TU):
        tok_pass(u).wait_send()
    for g in range(NG):
        out_far(g).wait_send()


def per_device(old_pieces, section_inputs, old_section_of, new_section_of, old_order, new_order):
    s = lax.axis_index("section")
    m = lax.axis_index("fsdp")
    pieces = old_pieces[0]
    tokens = section_inputs[0]
    _, rows, kv_width = pieces.shape
    tok_rows, width = tokens.shape
    layers = old_section_of.shape[0]
    cw, gw = kv_width // NC, kv_width // NG

    half_dim = HEAD_DIM // 2
    first = jnp.stack([m // 2 * tok_rows, (m // 2 + 8) % 16 * tok_rows])
    positions = first[:, None] + jnp.arange(tok_rows, dtype=jnp.int32)[None, :]
    freq_index = jnp.arange(half_dim, dtype=jnp.float32)
    inverse_freq = jnp.exp(freq_index * (-2.0 * math.log(500000.0) / HEAD_DIM))
    angles = positions.astype(jnp.float32)[:, :, None] * inverse_freq[None, None, :]
    cosine, sine = jnp.cos(angles), jnp.sin(angles)
    cos_in = jnp.concatenate([cosine, cosine], axis=-1)
    sin_in = jnp.concatenate([-sine, sine], axis=-1)

    dma = pltpu.SemaphoreType.DMA
    bf, fl = jnp.bfloat16, jnp.float32
    hbm = pl.BlockSpec(memory_space=pltpu.HBM)
    smem = pl.BlockSpec(memory_space=pltpu.SMEM)
    kv, shards = pl.pallas_call(
        body,
        out_shape=(jax.ShapeDtypeStruct((2, tok_rows, kv_width), bf),
                   jax.ShapeDtypeStruct((2 * rows, kv_width), bf)),
        in_specs=[smem] * 4 + [hbm] * 4,
        out_specs=(hbm, hbm),
        scratch_shapes=[
            pltpu.VMEM((NC, 2, rows, cw), bf),
            pltpu.VMEM((NC, 3, rows, cw), bf),
            pltpu.VMEM((NC, 4, rows, cw), bf),
            pltpu.VMEM((NC, 2, rows, cw), bf),
            pltpu.VMEM((NC, rows, cw), bf),
            pltpu.VMEM((NC, width, cw), bf),
            pltpu.VMEM((NC, 2 * rows, cw), bf),
            pltpu.VMEM((NC, 2 * rows, cw), bf),
            pltpu.VMEM((NC, 2 * rows, cw), bf),
            pltpu.VMEM((2, tok_rows, width), bf),
            pltpu.VMEM((2, tok_rows, gw), fl),
            pltpu.VMEM((NG, 2, tok_rows, gw), bf),
            pltpu.VMEM((2, tok_rows, HEAD_DIM), fl),
            pltpu.VMEM((2, tok_rows, HEAD_DIM), fl),
            dma((NC, 2)), dma((NC, 3)), dma((NC, 3)), dma((NC, 2)), dma((NC, 2)),
            dma((NC, 3)), dma((NC, 3)), dma((NC, 4)), dma((NC, 4)),
            dma((NC,)), dma((NC,)), dma((NC,)), dma((NC,)), dma((NC,)),
            dma((1,)), dma((4,)), dma((4,)), dma((2 * TU,)), dma((TU,)), dma((TU,)), dma((TU,)),
            dma((NG, 2)), dma((NG, 2)), dma((NG,)), dma((2,)),
        ],
        compiler_params=pltpu.CompilerParams(
            collective_id=0, has_side_effects=True, vmem_limit_bytes=66_000_000),
    )(old_section_of, new_section_of, old_order.reshape(-1), new_order.reshape(-1),
      pieces, tokens, cos_in, sin_in)

    ids = jnp.arange(layers, dtype=jnp.int32)
    own = ids == jnp.sum(jnp.where(new_section_of == 2 * s + m % 2, ids, 0))
    crossed = jnp.sum(jnp.where(own, old_section_of, 0)) // 2 != s // 2
    key_first = jnp.sum(jnp.where(own, old_order[:, 0], 0)) == crossed.astype(jnp.int32)
    joined = jnp.concatenate(
        [jnp.where(key_first, kv[0], kv[1]), jnp.where(key_first, kv[1], kv[0])], axis=-1)
    return shards[None], joined[None]


def solution(mesh):
    in_specs = (P("section", None, "fsdp", None), P("section", "fsdp", None), P(), P(), P(), P())
    out_specs = (P("section", "fsdp", None), P("section", "fsdp", None))
    return jax.shard_map(
        per_device, mesh=mesh, in_specs=in_specs, out_specs=out_specs, check_vma=False
    )
```

time: 667 us -> 196 us (0.29)
  waiting for transfers between devices: 472 us -> 0 us
  Pallas kernels: 0 us -> 177 us
  local copies, waits for them, and re-layouts: 72 us -> 4.88 us
  other arithmetic: 67.3 us -> 9.9 us
  matrix products: 21.7 us -> 0 us
  starting transfers between devices: 18.1 us -> 0 us
  between operations: 11.7 us -> 4.14 us
    ppermute x7 -> x0, waiting for transfers between devices: 455 us -> none  [from_partner(): return lax.ppermute(block, axis, route)]
    pallas_call x0 -> x1, Pallas kernels: none -> 177 us  [per_device(): pl.pallas_call(body, out_shape=(jax.ShapeDtypeStruct((2, tok_rows, kv_wid...]
    dynamic_slice x6 -> x0, local copies, waits for them, and re-layouts: 34 us -> none  [the longest x2 13.6 us: per_device(): lax.dynamic_index_in_dim(column_view, bit_value, axis_index, keepdims=False)]
    another operation x8 -> x1, other arithmetic: 33.3 us -> 0.08 us  [per_device(): first = jnp.stack([m // 2 * tok_rows, (m // 2 + 8) % 16 * tok_rows])]
    unnamed x18 -> x5, local copies, waits for them, and re-layouts: 32.9 us -> 3.66 us
    dot_general x1 -> x0, matrix products: 21.7 us -> none  [per_device(): jnp.einsum('tabi,saik->sbtk', token_blocks, gathered, preferred_element_t...]
    all_to_all x1 -> x0, waiting for transfers between devices: 17.6 us -> none  [per_device(): lax.all_to_all(outgoing, 'section', split_axis=0, concat_axis=0, tiled=True)]
    add x2 -> x0, other arithmetic: 16.4 us -> none  [per_device(): partial_value = mine + received]
  transfers between devices with their start and end apart: 8 -> 0, of which waited for: 6 -> 0; matrix products, arithmetic and copies ran while one was open for 12% -> 0% of each run, Pallas kernels for 0% -> 0%
where the time goes in v1:
time: 196 us
  Pallas kernels  177 us (90%)
  other arithmetic  9.9 us (5%)
  local copies, waits for them, and re-layouts  4.88 us (2%)
  between operations  4.14 us (2%)
    pallas_call x1, Pallas kernels, per_device(): pl.pallas_call(body, out_shape=(jax.ShapeDtypeStruct((2, tok_rows, kv_wid...  177 us

profile of v1, /device:TPU:1, one launch (start us, length us, event | category | flops | bytes accessed | tf_op | source)
XLA Modules:
  0.0 196.0 jit_solution(4340004052923604610)
XLA Ops:
  0.7 0.1 pad_add_fusion
  0.8 1.3 fusion.3
  2.1 2.1 %fusion.1 = (s32[]{:T(128)}, s32[]{:T(128)}) fusion(s32[8,2]{0,1:T(2,128)} %param.10, s32[]{:T(128)} %fusion.3, s32[8]{0:T(128)} %oldsec.1), kind=kLoop, calls=%fused_computation.12 | loop fusion | flops 38 | bytes 76 | tf_op jit(solution)/shard_map/reduce_sum | solution.py:498
  7.5 0.1 add_convert_fusion
  7.6 0.8 copy.11
  8.4 0.6 reshape.42.neword
  9.0 0.8 copy.10
  9.7 0.6 reshape.41.oldord
  10.3 1.9 fusion
  12.2 1.3 pad_maximum_fusion
  13.6 177.1 %shard_map.77 = (bf16[2,512,1024]{2,1,0:T(8,128)(2,1)}, bf16[1024,1024]{1,0:T(8,128)(2,1)}) custom-call(s32[8]{0:T(128)} %oldsec.1, s32[8]{0:T(128)} %newsec.1, s32[16]{0:T(128)} %reshape.41.oldord, s32[16]{0:T(128)} %reshape.42.neword, bf16[2,512,1024]{2,1,0:T(8,128)(2,1)} %bitcast.15, bf16[512,8192]{1,0:T(8,128)(2,1)} %bitcast.13, ...), custom_call_target="tpu_custom_call" | custom-call | tf_op jit(solution)/shard_map/pallas_call | solution.py:463
  190.6 1.7 select_bitcast_fusion.1
  192.3 0.0 copy-start
  192.3 1.5 maximum_bitcast_fusion
  193.8 0.8 copy-done
  194.7 1.3 copy.13
  (1 shorter events, 0.0 us)
Async XLA Ops:
  192.3 2.3 %copy-start = (bf16[1024,1024]{1,0:T(8,128)(2,1)S(1)}, bf16[1024,1024]{1,0:T(8,128)(2,1)}, u32[]{:S(2)}) copy-start(bf16[1024,1024]{1,0:T(8,128)(2,1)} %get-tuple-element.4) | copy-start | bytes 6291460

commit v2 on v1

v2 whole, which is shorter than its diff:
```python
import math

import jax
import jax.numpy as jnp
from jax import lax
from jax.experimental import pallas as pl
from jax.experimental.pallas import tpu as pltpu
from jax.sharding import PartitionSpec as P

HEAD_DIM = 128
MESH = pl.DeviceIdType.MESH
NC = 8
NG = 4
TU = 8
XF = 1
SPLIT = 192


def body(oldsec, newsec, oldord, neword, freq, pieces, tokens, kv_out, shard_out, flag_out,
         pc, og, cand, tb, gb, wb, n2, sha, shb, xb, acc, ob, ct, st,
         pc_sem, rs, rr, zs, zr, xs, xr, ns, nr, shl, shs, shr,
         tl, tas, tar, ts, tr, tfs, tfr, osm, orm, olm):
    rows = pieces.shape[1]
    cw = pieces.shape[2] // NC
    gw = pieces.shape[2] // NG
    per = NC // NG
    tok_rows, width = tokens.shape
    layers = oldsec.shape[0]
    s = lax.axis_index("section")
    m = lax.axis_index("fsdp")
    y = s // 2
    c = s % 2
    j = m // 16
    x = (m // 4) % 4
    z = m % 4
    h = z % 2
    zh = z // 2
    prob = (j + zh) % 2
    is_a = c == prob
    is_b = c != prob
    alone = jnp.logical_and(c == j, zh == 0)
    not_alone = jnp.logical_or(c != j, zh != 0)

    def dev(yy, cc, jj, xx, zz):
        return (2 * yy + cc, jj * 16 + xx * 4 + zz)

    core_dev = dev(y, 1 - c, j, x, z)
    cross_dev = [dev(1 - y, k, 1 - j, x, z) for k in range(2)]
    zf = (z + 2) % 4
    xp, xm, xf = (x + 1) % 4, (x + 3) % 4, (x + 2) % 4
    xp_dev, xm_dev = (dev(y, c, j, xx, z) for xx in (xp, xm))

    def remote(src, dst, send, recv, device):
        return pltpu.make_async_remote_copy(
            src_ref=src, dst_ref=dst, send_sem=send, recv_sem=recv,
            device_id=device, device_id_type=MESH)

    def arrived(dst, send, recv, device):
        remote(dst, dst, send, recv, device).wait_recv()

    def pc_copy(i, a):
        return pltpu.make_async_copy(
            pieces.at[a, :, pl.ds(i * cw, cw)], pc.at[i, a], pc_sem.at[i, a])

    for i in range(NC):
        for a in range(2):
            pc_copy(i, a).start()

    def layer_of(section):
        found = jnp.int32(0)
        for l in range(layers):
            found = found + jnp.where(newsec[l] == section, l, 0)
        return found

    def entry(table, layer):
        found = jnp.int32(0)
        for l in range(layers):
            found = found + jnp.where(layer == l, table(l), 0)
        return found

    high = jnp.int32(0)
    for l in range(layers):
        high = jnp.where(oldsec[l] == s, l, high)
    row_high = entry(lambda l: newsec[l], high) // 2
    source = [entry(lambda l: oldsec[l], layer_of(2 * s + k)) for k in range(2)]
    gl = layer_of(2 * (2 * y + prob) + h)
    gl_crossed = jnp.where(entry(lambda l: oldsec[l], gl) // 2 == y, 0, 1)
    gl_old = entry(lambda l: oldord[0, l], gl)
    gl_new = entry(lambda l: neword[0, l], gl)
    gl_turn = (jnp.where(gl_old == gl_new, 0, 1) + gl_crossed + j + c) % 2
    is_key = gl_old == (c + gl_crossed) % 2
    ol = layer_of(2 * s + h)
    ol_crossed = jnp.where(entry(lambda l: oldsec[l], ol) // 2 == y, 0, 1)
    key_at = (entry(lambda l: oldord[0, l], ol) + ol_crossed) % 2
    flag_out[...] = jnp.zeros_like(flag_out) + key_at

    barrier = pltpu.get_barrier_semaphore()
    partners = cross_dev + [xp_dev, xm_dev]
    for n in range(1, 16):
        partners.append(dev(y, (c + n) % 2, (j + n // 2) % 2, x, (z + n // 4) % 4))
    for device in partners:
        pl.semaphore_signal(barrier, inc=1, device_id=device, device_id_type=MESH)
    pl.semaphore_wait(barrier, len(partners))

    tok_step = width // (2 * TU)
    quarter = width // 4

    def tok_send(v):
        u, a = v // 2, v % 2
        cols = pl.ds((a * TU + u) * tok_step, tok_step)
        parts = [(pl.ds(0, SPLIT), dev(y, a, 1 - j, x, z)),
                 (pl.ds(SPLIT, tok_rows - SPLIT), dev(y, a, j, x, zf))]
        return [remote(tokens.at[part, cols], xb.at[1, part, cols], ts.at[v, k], tr.at[u, k], device)
                for k, (part, device) in enumerate(parts)]

    def tok_here(u):
        cols = pl.ds(pl.multiple_of((c * TU + u) * tok_step, 128), tok_step)
        for k, part in enumerate((pl.ds(0, SPLIT), pl.ds(SPLIT, tok_rows - SPLIT))):
            arrived(xb.at[1, part, cols], tfs.at[u], tr.at[u, k], core_dev)

    def tok_pass(u):
        cols = pl.ds(pl.multiple_of((c * TU + u) * tok_step, 128), tok_step)
        return remote(xb.at[1, :, cols], xb.at[1, :, cols], tfs.at[u], tfr.at[u], core_dev)

    def tok_other(u):
        cols = pl.ds(pl.multiple_of(((1 - c) * TU + u) * tok_step, 128), tok_step)
        return remote(xb.at[1, :, cols], xb.at[1, :, cols], tfs.at[u], tfr.at[u], core_dev)

    def tok_core(k):
        cols = pl.ds(k * quarter, quarter)
        return remote(tokens.at[:, cols], xb.at[0, :, cols], tas.at[k], tar.at[k], core_dev)

    tok_local = pltpu.make_async_copy(tokens, xb.at[0], tl.at[0])
    tok_next = [0]

    def send_tokens(count):
        take = range(tok_next[0], min(tok_next[0] + count, 2 * TU))
        tok_next[0] += len(take)

        @pl.when(is_b)
        def _():
            for v in take:
                for copy in tok_send(v):
                    copy.start()

    def relay_copies(i):
        return [remote(og.at[i, k], cand.at[i, s], rs.at[i, k],
                       rr.at[i, 0] if k == 0 else rr.at[i, 1 + c], device)
                for k, device in enumerate([core_dev] + cross_dev)]

    relay_rows = [2 * y + 1 - c, 2 * (1 - y), 2 * (1 - y) + 1]

    def relay_send(i):
        for a in range(2):
            pc_copy(i, a).wait()

        def tile(t, carry):
            part = pl.ds(pl.multiple_of(t * 128, 128), 128)
            low_rows = pc[i, 0, part, :]
            high_rows = pc[i, 1, part, :]
            for k in range(3):
                og[i, k, part, :] = jnp.where(row_high == relay_rows[k], high_rows, low_rows)
            cand[i, s, part, :] = jnp.where(row_high == s, high_rows, low_rows)
            return carry

        lax.fori_loop(0, rows // 128, tile, 0)
        for copy in relay_copies(i):
            copy.start()

    slots = [x, xm, xp, xf]

    def place(slot, zz):
        return pl.ds(pl.multiple_of((slots[slot] * 4 + zz) * rows, rows), rows)

    def spread(i, slot):
        copies = []
        for k in range(2):
            src = gb.at[i, slots[slot], k] if i < XF else tb.at[i, k]
            target = 2 * ((c + j) % 2) + k
            for far in (1, 0):
                device = dev(y, j, (j + far) % 2, x, (target + 2 * far) % 4)
                copy = remote(src, wb.at[i, place(slot, z)], zs.at[i, slot, 2 * k + far],
                              zr.at[i, slot, z], device)
                here = jnp.logical_and(alone, h == k)
                copies.append((copy, None if far else jnp.logical_not(here)))
        return copies

    def spread_each(i, slot, act):
        for copy, needed in spread(i, slot):
            if needed is None:
                act(copy)
            else:
                @pl.when(needed)
                def _():
                    act(copy)

    def spread_start(i, slot):
        spread_each(i, slot, lambda copy: copy.start())

    def spread_arrived(i, slot):
        for n in range(1, 4):
            zz = (z + n) % 4
            arrived(wb.at[i, place(slot, zz)], zs.at[i, slot, 0], zr.at[i, slot, zz], core_dev)

        @pl.when(not_alone)
        def _():
            arrived(wb.at[i, place(slot, z)], zs.at[i, slot, 0], zr.at[i, slot, z], core_dev)

    def keep_first(i, slot):
        @pl.when(alone)
        def _():
            def tile(t, carry):
                part = pl.ds(pl.multiple_of(t * 128, 128), 128)
                to = pl.ds(pl.multiple_of((slots[slot] * 4 + z) * rows + t * 128, 128), 128)
                wb[i, to, :] = gb[i, slots[slot], h, part, :]
                return carry

            lax.fori_loop(0, rows // 128, tile, 0)

    def choose(i):
        arrived(cand.at[i, 2 * y + 1 - c], rs.at[i, 0], rr.at[i, 0], core_dev)
        for k in range(2):
            arrived(cand.at[i, 2 * (1 - y) + k], rs.at[i, 1 + k], rr.at[i, 1 + k], cross_dev[k])

        def tile(t, carry):
            part = pl.ds(pl.multiple_of(t * 128, 128), 128)
            four = [cand[i, k, part, :] for k in range(4)]
            for k in range(2):
                want = source[k]
                value = jnp.where(want < 2, jnp.where(want == 0, four[0], four[1]),
                                  jnp.where(want == 2, four[2], four[3]))
                if i < XF:
                    gb[i, x, k, part, :] = value
                else:
                    tb[i, k, part, :] = value
            return carry

        lax.fori_loop(0, rows // 128, tile, 0)
        if i < XF:
            for copy in first_own(i):
                copy.start()
        spread_start(i, 0)
        if i < XF:
            keep_first(i, 0)
        else:
            @pl.when(alone)
            def _():
                def keep(t, carry):
                    part = pl.ds(pl.multiple_of(t * 128, 128), 128)
                    to = pl.ds(pl.multiple_of((x * 4 + z) * rows + t * 128, 128), 128)
                    wb[i, to, :] = tb[i, h, part, :]
                    return carry

                lax.fori_loop(0, rows // 128, keep, 0)

    def first_own(i):
        mine = gb.at[i, x]
        return [remote(mine, mine, xs.at[i, 0], xr.at[i, 0], xp_dev),
                remote(mine, mine, xs.at[i, 1], xr.at[i, 1], xm_dev)]

    def first_pass_copies(i):
        left, right = gb.at[i, xm, 0], gb.at[i, xp, 1]
        return [remote(left, left, xs.at[i, 2], xr.at[i, 2], xp_dev),
                remote(right, right, xs.at[i, 3], xr.at[i, 3], xm_dev)]

    def first_pass(i):
        arrived(gb.at[i, xm], xs.at[i, 0], xr.at[i, 0], xp_dev)
        arrived(gb.at[i, xp], xs.at[i, 1], xr.at[i, 1], xm_dev)
        for copy in first_pass_copies(i):
            copy.start()
        for slot in (1, 2):
            spread_start(i, slot)
            keep_first(i, slot)

    def first_far(i):
        arrived(gb.at[i, xf, 0], xs.at[i, 2], xr.at[i, 2], xp_dev)
        arrived(gb.at[i, xf, 1], xs.at[i, 3], xr.at[i, 3], xm_dev)
        spread_start(i, 3)
        keep_first(i, 3)

    def block(i, xx, first, count):
        return wb.at[i, pl.ds(pl.multiple_of(xx * 4 * rows + first, rows), count)]

    def own_copies(i):
        mine = block(i, x, 0, 4 * rows)
        return [remote(mine, mine, xs.at[i, 0], xr.at[i, 0], xp_dev),
                remote(mine, mine, xs.at[i, 1], xr.at[i, 1], xm_dev)]

    def pass_copies(i):
        left = block(i, xm, 0, 2 * rows)
        right = block(i, xp, 2 * rows, 2 * rows)
        return [remote(left, left, xs.at[i, 2], xr.at[i, 2], xp_dev),
                remote(right, right, xs.at[i, 3], xr.at[i, 3], xm_dev)]

    pair = pl.ds(pl.multiple_of((x * 4 + z // 2 * 2) * rows, rows), 2 * rows)

    def near_copy(i):
        return remote(wb.at[i, pair], n2.at[i], ns.at[i], nr.at[i], core_dev)

    def x_own(i):
        spread_arrived(i, 0)
        if i >= XF:
            for copy in own_copies(i):
                copy.start()

        @pl.when(is_b)
        def _():
            near_copy(i).start()

    def x_pass(i):
        arrived(block(i, xm, 0, 4 * rows), xs.at[i, 0], xr.at[i, 0], xp_dev)
        first, second = pass_copies(i)
        first.start()
        arrived(block(i, xp, 0, 4 * rows), xs.at[i, 1], xr.at[i, 1], xm_dev)
        second.start()

    def far_arrived(i):
        if i < XF:
            for slot in (1, 2, 3):
                spread_arrived(i, slot)
            return
        arrived(block(i, xf, 0, 2 * rows), xs.at[i, 2], xr.at[i, 2], xp_dev)
        arrived(block(i, xf, 2 * rows, 2 * rows), xs.at[i, 3], xr.at[i, 3], xm_dev)

    def shard_local(i):
        return pltpu.make_async_copy(sha.at[i], shard_out.at[:, pl.ds(i * cw, cw)], shl.at[i])

    def shard_far(i):
        return remote(shb.at[i], shard_out.at[:, pl.ds(i * cw, cw)], shs.at[i], shr.at[i],
                      dev(y, c, 1 - j, x, z))

    def shard(i):
        @pl.when(is_a)
        def _():
            near_copy(i).wait_recv()

            def tile(t, carry):
                part = pl.ds(pl.multiple_of(t * 128, 128), 128)
                near = pl.ds(pl.multiple_of((x * 4 + z // 2 * 2) * rows + t * 128, 128), 128)
                mine = wb[i, near, :]
                other = n2[i, part, :]
                sha[i, part, :] = jnp.where(gl_turn == 0, mine, other)
                shb[i, part, :] = jnp.where(gl_turn == 0, other, mine)
                return carry

            lax.fori_loop(0, 2 * rows // 128, tile, 0)

    def shard_send(i):
        @pl.when(is_a)
        def _():
            shard_local(i).start()
            shard_far(i).start()

    def multiply(g, xx, half):
        first = pl.multiple_of(xx * 4 * rows + half * 2 * rows, 2 * rows)
        ks = pl.ds(first, 2 * rows)
        weight = jnp.concatenate([wb[per * g + k, ks, :] for k in range(per)], axis=1)
        for slot in range(2):
            acc[slot] += jnp.dot(xb[slot, :, ks], weight, preferred_element_type=jnp.float32)

    def finish(g):
        def tile(t, carry):
            part = pl.ds(pl.multiple_of(t * 64, 64), 64)
            for slot in range(2):
                cosine = ct[slot, part, :]
                sine = st[slot, part, :]
                for head in range(gw // HEAD_DIM):
                    cols = slice(head * HEAD_DIM, (head + 1) * HEAD_DIM)
                    value = acc[slot, part, cols]
                    turned = value * cosine + pltpu.roll(value, HEAD_DIM // 2, 1) * sine
                    ob[g, slot, part, cols] = turned.astype(jnp.bfloat16)
            return carry

        lax.fori_loop(0, tok_rows // 64, tile, 0)

    def out_local(g):
        return pltpu.make_async_copy(
            ob.at[g, 0], kv_out.at[c, :, pl.ds(g * gw, gw)], olm.at[g])

    def out_near(g):
        return remote(ob.at[g, 0], kv_out.at[c, :, pl.ds(g * gw, gw)],
                      osm.at[g, 0], orm.at[g, c], core_dev)

    def out_parts(g, q):
        cols = pl.ds(g * gw, gw)
        return [kv_out.at[q, pl.ds(0, SPLIT), cols],
                kv_out.at[q, pl.ds(SPLIT, tok_rows - SPLIT), cols]]

    def out_far(g):
        to_y, to_z = out_parts(g, c)
        return [remote(ob.at[g, 1, pl.ds(0, SPLIT)], to_y, osm.at[g, 1], orm.at[g, c],
                       dev(y, prob, 1 - j, x, z)),
                remote(ob.at[g, 1, pl.ds(SPLIT, tok_rows - SPLIT)], to_z, osm.at[g, 2],
                       orm.at[g, 2 + c], dev(y, prob, j, x, zf))]

    def out_send(g):
        for copy in out_far(g):
            copy.start()

        @pl.when(is_a)
        def _():
            out_local(g).start()

        @pl.when(is_b)
        def _():
            out_near(g).start()

    def tables():
        first = m // 2 * tok_rows
        by_y = (m // 2 + 8) % 16 * tok_rows
        by_z = (m // 2 + 1 - 2 * zh) * tok_rows
        lane = lax.broadcasted_iota(jnp.int32, (64, HEAD_DIM), 1)
        row = lax.broadcasted_iota(jnp.int32, (64, HEAD_DIM), 0)

        def tile(t, carry):
            part = pl.ds(pl.multiple_of(t * 64, 64), 64)
            for slot in range(2):
                base = first if slot == 0 else jnp.where(t * 64 < SPLIT, by_y, by_z)
                position = (base + t * 64 + row).astype(jnp.float32)
                angle = position * freq[0:1, :]
                sine = jnp.sin(angle)
                sine = jnp.where(lane < HEAD_DIM // 2, -sine, sine)
                ct[slot, part, :] = jnp.where(is_key, jnp.cos(angle), 1.0)
                st[slot, part, :] = jnp.where(is_key, sine, 0.0)
            return carry

        lax.fori_loop(0, tok_rows // 64, tile, 0)

    send_tokens(2)
    for i in range(NC):
        relay_send(i)
    for t in range(NC + 1):
        if t < NC:
            choose(t)
            if t >= 1:
                send_tokens(2)
        if t == 0:
            @pl.when(is_a)
            def _():
                tok_local.start()
                for k in range(4):
                    tok_core(k).start()
        if 0 < t <= XF:
            first_pass(t - 1)
        if t >= 1 and t - 1 >= XF:
            x_own(t - 1)
        if 2 <= t < 2 + XF:
            first_far(t - 2)
            x_own(t - 2)
    send_tokens(2 * TU)
    tables()
    for i in range(NC):
        if i >= XF:
            x_pass(i)
        shard(i)
        if i >= 2:
            tok_here(i - 2)
            tok_pass(i - 2).start()
    for u in range(NC - 2, TU):
        tok_here(u)
        tok_pass(u).start()
    for i in range(NC):
        shard_send(i)

    @pl.when(is_a)
    def _():
        tok_local.wait()

    @pl.when(is_b)
    def _():
        for k in range(4):
            tok_core(k).wait_recv()

    for u in range(TU):
        tok_other(u).wait_recv()

    for g in range(NG):
        acc[...] = jnp.zeros_like(acc)

        def near_block(t, carry):
            b = t // 2
            multiply(g, (x + b + b // 2) % 4, t % 2)
            return carry

        for k in range(per):
            if per * g + k < XF:
                far_arrived(per * g + k)
        lax.fori_loop(0, 6, near_block, 0)
        for k in range(per):
            if per * g + k >= XF:
                far_arrived(per * g + k)

        def far_block(t, carry):
            multiply(g, xf, t)
            return carry

        lax.fori_loop(0, 2, far_block, 0)
        finish(g)
        out_send(g)

    for i in range(NC):
        for copy in relay_copies(i):
            copy.wait_send()
        for copy in (first_own(i) + first_pass_copies(i) if i < XF else own_copies(i) + pass_copies(i)):
            copy.wait_send()
        for slot in range(4 if i < XF else 1):
            spread_each(i, slot, lambda copy: copy.wait_send())

    @pl.when(is_a)
    def _():
        for k in range(4):
            tok_core(k).wait_send()
        for i in range(NC):
            shard_local(i).wait()
            shard_far(i).wait_send()
        for g in range(NG):
            out_local(g).wait()
            arrived(kv_out.at[1 - c, :, pl.ds(g * gw, gw)], osm.at[g, 0], orm.at[g, 1 - c], core_dev)

    @pl.when(is_b)
    def _():
        for v in range(2 * TU):
            for copy in tok_send(v):
                copy.wait_send()
        for i in range(NC):
            near_copy(i).wait_send()
            shard_far(i).wait_recv()
        for g in range(NG):
            out_near(g).wait_send()
            for q in range(2):
                for k, part in enumerate(out_parts(g, q)):
                    arrived(part, osm.at[g, 0], orm.at[g, 2 * k + q], core_dev)

    for u in range(TU):
        tok_pass(u).wait_send()
    for g in range(NG):
        for copy in out_far(g):
            copy.wait_send()


def per_device(old_pieces, section_inputs, old_section_of, new_section_of, old_order, new_order):
    pieces = old_pieces[0]
    tokens = section_inputs[0]
    _, rows, kv_width = pieces.shape
    tok_rows, width = tokens.shape
    cw, gw = kv_width // NC, kv_width // NG

    half_dim = HEAD_DIM // 2
    freq_index = (jnp.arange(HEAD_DIM, dtype=jnp.int32) % half_dim).astype(jnp.float32)
    inverse_freq = jnp.exp(freq_index * (-2.0 * math.log(500000.0) / HEAD_DIM))
    freq = jnp.broadcast_to(inverse_freq[None, :], (8, HEAD_DIM))

    dma = pltpu.SemaphoreType.DMA
    bf, fl = jnp.bfloat16, jnp.float32
    hbm = pl.BlockSpec(memory_space=pltpu.HBM)
    vmem = pl.BlockSpec(memory_space=pltpu.VMEM)
    smem = pl.BlockSpec(memory_space=pltpu.SMEM)
    kv, shards, flag = pl.pallas_call(
        body,
        out_shape=(jax.ShapeDtypeStruct((2, tok_rows, kv_width), bf),
                   jax.ShapeDtypeStruct((2 * rows, kv_width), bf),
                   jax.ShapeDtypeStruct((8, 128), jnp.int32)),
        in_specs=[smem] * 4 + [vmem] + [hbm] * 2,
        out_specs=(hbm, hbm, vmem),
        scratch_shapes=[
            pltpu.VMEM((NC, 2, rows, cw), bf),
            pltpu.VMEM((NC, 3, rows, cw), bf),
            pltpu.VMEM((NC, 4, rows, cw), bf),
            pltpu.VMEM((NC, 2, rows, cw), bf),
            pltpu.VMEM((max(XF, 1), 4, 2, rows, cw), bf),
            pltpu.VMEM((NC, width, cw), bf),
            pltpu.VMEM((NC, 2 * rows, cw), bf),
            pltpu.VMEM((NC, 2 * rows, cw), bf),
            pltpu.VMEM((NC, 2 * rows, cw), bf),
            pltpu.VMEM((2, tok_rows, width), bf),
            pltpu.VMEM((2, tok_rows, gw), fl),
            pltpu.VMEM((NG, 2, tok_rows, gw), bf),
            pltpu.VMEM((2, tok_rows, HEAD_DIM), fl),
            pltpu.VMEM((2, tok_rows, HEAD_DIM), fl),
            dma((NC, 2)), dma((NC, 3)), dma((NC, 3)),
            dma((NC, 4, 4)), dma((NC, 4, 4)), dma((NC, 4)), dma((NC, 4)),
            dma((NC,)), dma((NC,)), dma((NC,)), dma((NC,)), dma((NC,)),
            dma((1,)), dma((4,)), dma((4,)), dma((2 * TU, 2)), dma((TU, 2)), dma((TU,)), dma((TU,)),
            dma((NG, 3)), dma((NG, 4)), dma((NG,)),
        ],
        compiler_params=pltpu.CompilerParams(
            collective_id=0, has_side_effects=True, vmem_limit_bytes=66_000_000),
    )(old_section_of, new_section_of, old_order.T, new_order.T, freq, pieces, tokens)

    swapped = flag[0, 0] == 1
    joined = jnp.where(swapped, jnp.concatenate([kv[1], kv[0]], axis=-1),
                       jnp.concatenate([kv[0], kv[1]], axis=-1))
    return shards[None], joined[None]


def solution(mesh):
    in_specs = (P("section", None, "fsdp", None), P("section", "fsdp", None), P(), P(), P(), P())
    out_specs = (P("section", "fsdp", None), P("section", "fsdp", None))
    return jax.shard_map(
        per_device, mesh=mesh, in_specs=in_specs, out_specs=out_specs, check_vma=False
    )
```

time: 196 us -> 197 us (level)
  Pallas kernels: 177 us -> 188 us
  other arithmetic: 9.9 us -> 2.12 us
  between operations: 4.14 us -> 1.31 us
    pallas_call x1, Pallas kernels: 177 us -> 188 us  [per_device(): pl.pallas_call(body, out_shape=(jax.ShapeDtypeStruct((2, tok_rows, kv_wid...]
    reduce_sum x2 -> x0, other arithmetic: 3.34 us -> none  [the longest x1 2.05 us: per_device(): jnp.sum(jnp.where(own, old_order[:, 0], 0)) == crossed.astype(jnp.int32)]
    slice x0 -> x2, local copies, waits for them, and re-layouts: none -> 2.91 us  [the longest x1 1.71 us: per_device(): kv[1]]
    unnamed x5 -> x3, local copies, waits for them, and re-layouts: 3.66 us -> 1.32 us
where the time goes in v2:
time: 197 us; the launch traced here: 196 us
  Pallas kernels  188 us (95%)
  local copies, waits for them, and re-layouts  4.83 us (2%)
  other arithmetic  2.12 us (1%)
    pallas_call x1, Pallas kernels, per_device(): pl.pallas_call(body, out_shape=(jax.ShapeDtypeStruct((2, tok_rows, kv_wid...  188 us

profile of v2, /device:TPU:1, one launch (start us, length us, event | category | flops | bytes accessed | tf_op | source)
XLA Modules:
  0.0 196.4 jit_solution(15535766546529214236)
XLA Ops:
  0.6 0.6 broadcast_in_dim.4.freq
  1.2 188.1 %shard_map.77 = (bf16[2,512,1024]{2,1,0:T(8,128)(2,1)}, bf16[1024,1024]{1,0:T(8,128)(2,1)}, s32[8,128]{1,0:T(8,128)}) custom-call(s32[8]{0:T(128)} %oldsec.1, s32[8]{0:T(128)} %newsec.1, s32[2,8]{1,0:T(2,128)} %bitcast.9, s32[2,8]{1,0:T(2,128)} %bitcast.10, f32[8,128]{1,0:T(8,128)} %broadcast_in_dim.4.freq, bf16[2,512,1024]{2,1,0:T(8,128)(2,1)} %bitcast.8, ...), custom_call_target="tpu_custom_call" | custom-call | tf_op jit(solution)/shard_map/pallas_call | solution.py:558
  189.4 1.2 slice.11
  191.2 1.7 fusion.3
  192.9 0.0 copy-start
  192.9 2.1 %maximum_select_fusion = bf16[1,512,2048]{2,1,0:T(8,128)(2,1)} fusion(bf16[1,512,1024]{2,1,0:T(8,128)(2,1)S(1)} %get-tuple-element.9, bf16[1,512,1024]{2,1,0:T(8,128)(2,1)S(1)} %get-tuple-element.8, pred[]{:T(512)} %bitcast.5), kind=kLoop, calls=%fused_computation | loop fusion | flops 9437184 | bytes 4194305 | tf_op jit(solution)/shard_map/jit(_where)/select_n | solution.py:591
  195.1 0.0 copy-done
  195.1 1.3 copy.9
  (1 shorter events, 0.0 us)
Async XLA Ops:
  192.9 2.1 %copy-start = (bf16[1024,1024]{1,0:T(8,128)(2,1)S(1)}, bf16[1024,1024]{1,0:T(8,128)(2,1)}, u32[]{:S(2)}) copy-start(bf16[1024,1024]{1,0:T(8,128)(2,1)} %get-tuple-element.5) | copy-start | bytes 6291460

commit v3 on v2

--- a/solution.py
+++ b/solution.py
@@ -268,15 +268,13 @@
         arrived(gb.at[i, xp], xs.at[i, 1], xr.at[i, 1], xm_dev)
         for copy in first_pass_copies(i):
             copy.start()
-        for slot in (1, 2):
-            spread_start(i, slot)
-            keep_first(i, slot)
 
     def first_far(i):
         arrived(gb.at[i, xf, 0], xs.at[i, 2], xr.at[i, 2], xp_dev)
         arrived(gb.at[i, xf, 1], xs.at[i, 3], xr.at[i, 3], xm_dev)
-        spread_start(i, 3)
-        keep_first(i, 3)
+        for slot in (1, 2, 3):
+            spread_start(i, slot)
+            keep_first(i, slot)
 
     def block(i, xx, first, count):
         return wb.at[i, pl.ds(pl.multiple_of(xx * 4 * rows + first, rows), count)]
@@ -351,12 +349,30 @@
             shard_local(i).start()
             shard_far(i).start()
 
-    def multiply(g, xx, half):
+    def multiply(g, slots_now, xx, half):
         first = pl.multiple_of(xx * 4 * rows + half * 2 * rows, 2 * rows)
         ks = pl.ds(first, 2 * rows)
         weight = jnp.concatenate([wb[per * g + k, ks, :] for k in range(per)], axis=1)
-        for slot in range(2):
-            acc[slot] += jnp.dot(xb[slot, :, ks], weight, preferred_element_type=jnp.float32)
+        for slot in slots_now:
+            acc[g, slot] += jnp.dot(xb[slot, :, ks], weight, preferred_element_type=jnp.float32)
+
+    def near(g, slots_now):
+        for slot in slots_now:
+            acc[g, slot] = jnp.zeros(acc.shape[2:], acc.dtype)
+
+        def near_block(t, carry):
+            b = t // 2
+            multiply(g, slots_now, (x + b + b // 2) % 4, t % 2)
+            return carry
+
+        lax.fori_loop(0, 6, near_block, 0)
+
+    def far(g):
+        def far_block(t, carry):
+            multiply(g, (0, 1), xf, t)
+            return carry
+
+        lax.fori_loop(0, 2, far_block, 0)
 
     def finish(g):
         def tile(t, carry):
@@ -366,7 +382,7 @@
                 sine = st[slot, part, :]
                 for head in range(gw // HEAD_DIM):
                     cols = slice(head * HEAD_DIM, (head + 1) * HEAD_DIM)
-                    value = acc[slot, part, cols]
+                    value = acc[g, slot, part, cols]
                     turned = value * cosine + pltpu.roll(value, HEAD_DIM // 2, 1) * sine
                     ob[g, slot, part, cols] = turned.astype(jnp.bfloat16)
             return carry
@@ -426,41 +442,41 @@
 
         lax.fori_loop(0, tok_rows // 64, tile, 0)
 
+    def token_pass(u):
+        tok_here(u)
+        tok_pass(u).start()
+
     send_tokens(2)
     for i in range(NC):
         relay_send(i)
-    for t in range(NC + 1):
-        if t < NC:
-            choose(t)
-            if t >= 1:
-                send_tokens(2)
-        if t == 0:
-            @pl.when(is_a)
-            def _():
-                tok_local.start()
-                for k in range(4):
-                    tok_core(k).start()
-        if 0 < t <= XF:
-            first_pass(t - 1)
-        if t >= 1 and t - 1 >= XF:
-            x_own(t - 1)
-        if 2 <= t < 2 + XF:
-            first_far(t - 2)
-            x_own(t - 2)
+    choose(0)
+
+    @pl.when(is_a)
+    def _():
+        tok_local.start()
+        for k in range(4):
+            tok_core(k).start()
+
+    choose(1)
+    first_pass(0)
+    choose(2)
+    x_own(1)
+    choose(3)
+    x_own(2)
+    choose(4)
+    x_own(3)
+    choose(5)
+    x_own(4)
+    x_pass(1)
+    choose(6)
+    x_own(5)
+    choose(7)
     send_tokens(2 * TU)
+    x_own(6)
+    x_pass(2)
+    x_own(7)
     tables()
-    for i in range(NC):
-        if i >= XF:
-            x_pass(i)
-        shard(i)
-        if i >= 2:
-            tok_here(i - 2)
-            tok_pass(i - 2).start()
-    for u in range(NC - 2, TU):
-        tok_here(u)
-        tok_pass(u).start()
-    for i in range(NC):
-        shard_send(i)
+    x_own(0)
 
     @pl.when(is_a)
     def _():
@@ -471,30 +487,39 @@
         for k in range(4):
             tok_core(k).wait_recv()
 
+    x_pass(3)
+    for i in range(0, 4):
+        shard(i)
+        shard_send(i)
+    near(1, (0,))
+    token_pass(0)
+    token_pass(1)
+    x_pass(4)
+    token_pass(2)
+    token_pass(3)
+    x_pass(5)
+    first_far(0)
+    for i in range(4, 8):
+        shard(i)
+        shard_send(i)
+    near(2, (0,))
+    token_pass(4)
+    x_pass(6)
+    token_pass(5)
+    token_pass(6)
+    token_pass(7)
+    x_pass(7)
+    near(3, (0,))
     for u in range(TU):
         tok_other(u).wait_recv()
-
-    for g in range(NG):
-        acc[...] = jnp.zeros_like(acc)
-
-        def near_block(t, carry):
-            b = t // 2
-            multiply(g, (x + b + b // 2) % 4, t % 2)
-            return carry
-
+    for g in (1, 2, 3):
+        near(g, (1,))
+    for g in (1, 2, 0, 3):
         for k in range(per):
-            if per * g + k < XF:
-                far_arrived(per * g + k)
-        lax.fori_loop(0, 6, near_block, 0)
-        for k in range(per):
-            if per * g + k >= XF:
-                far_arrived(per * g + k)
-
-        def far_block(t, carry):
-            multiply(g, xf, t)
-            return carry
-
-        lax.fori_loop(0, 2, far_block, 0)
+            far_arrived(per * g + k)
+        if g == 0:
+            near(g, (0, 1))
+        far(g)
         finish(g)
         out_send(g)
 
@@ -573,7 +598,7 @@
             pltpu.VMEM((NC, 2 * rows, cw), bf),
             pltpu.VMEM((NC, 2 * rows, cw), bf),
             pltpu.VMEM((2, tok_rows, width), bf),
-            pltpu.VMEM((2, tok_rows, gw), fl),
+            pltpu.VMEM((NG, 2, tok_rows, gw), fl),
             pltpu.VMEM((NG, 2, tok_rows, gw), bf),
             pltpu.VMEM((2, tok_rows, HEAD_DIM), fl),
             pltpu.VMEM((2, tok_rows, HEAD_DIM), fl),

time: 197 us -> 175 us (0.89)
  Pallas kernels: 188 us -> 166 us
    pallas_call x1, Pallas kernels: 188 us -> 166 us  [per_device(): pl.pallas_call(body, out_shape=(jax.ShapeDtypeStruct((2, tok_rows, kv_wid...]
where the time goes in v3:
time: 175 us; the launch traced here: 174 us
  Pallas kernels  166 us (95%)
  local copies, waits for them, and re-layouts  4.83 us (3%)
  other arithmetic  2.12 us (1%)
    pallas_call x1, Pallas kernels, per_device(): pl.pallas_call(body, out_shape=(jax.ShapeDtypeStruct((2, tok_rows, kv_wid...  166 us

profile of v3, /device:TPU:1, one launch (start us, length us, event | category | flops | bytes accessed | tf_op | source)
XLA Modules:
  0.0 174.3 jit_solution(6705745162171599517)
XLA Ops:
  0.6 0.6 broadcast_in_dim.4.freq
  1.2 166.1 %shard_map.77 = (bf16[2,512,1024]{2,1,0:T(8,128)(2,1)}, bf16[1024,1024]{1,0:T(8,128)(2,1)}, s32[8,128]{1,0:T(8,128)}) custom-call(s32[8]{0:T(128)} %oldsec.1, s32[8]{0:T(128)} %newsec.1, s32[2,8]{1,0:T(2,128)} %bitcast.9, s32[2,8]{1,0:T(2,128)} %bitcast.10, f32[8,128]{1,0:T(8,128)} %broadcast_in_dim.4.freq, bf16[2,512,1024]{2,1,0:T(8,128)(2,1)} %bitcast.8, ...), custom_call_target="tpu_custom_call" | custom-call | tf_op jit(solution)/shard_map/pallas_call | solution.py:583
  167.3 1.2 slice.11
  169.2 1.7 fusion.3
  170.9 0.0 copy-start
  170.9 2.1 %maximum_select_fusion = bf16[1,512,2048]{2,1,0:T(8,128)(2,1)} fusion(bf16[1,512,1024]{2,1,0:T(8,128)(2,1)S(1)} %get-tuple-element.9, bf16[1,512,1024]{2,1,0:T(8,128)(2,1)S(1)} %get-tuple-element.8, pred[]{:T(512)} %bitcast.5), kind=kLoop, calls=%fused_computation | loop fusion | flops 9437184 | bytes 4194305 | tf_op jit(solution)/shard_map/jit(_where)/select_n | solution.py:616
  173.0 0.0 copy-done
  173.0 1.3 copy.9
  (1 shorter events, 0.0 us)
Async XLA Ops:
  170.9 2.1 %copy-start = (bf16[1024,1024]{1,0:T(8,128)(2,1)S(1)}, bf16[1024,1024]{1,0:T(8,128)(2,1)}, u32[]{:S(2)}) copy-start(bf16[1024,1024]{1,0:T(8,128)(2,1)} %get-tuple-element.5) | copy-start | bytes 6291460

commit v4 on v3

v4 whole, which is shorter than its diff:
```python
import math

import jax
import jax.numpy as jnp
from jax import lax
from jax.experimental import pallas as pl
from jax.experimental.pallas import tpu as pltpu
from jax.sharding import PartitionSpec as P

HEAD_DIM = 128
MESH = pl.DeviceIdType.MESH
NC = 8
NG = 4
TU = 8
SPLIT = 192


def body(oldsec, newsec, oldord, neword, freq, pieces, tokens, kv_out, shard_out,
         px, pc, og, cand, gb, wb, n2, sha, shb, xb, acc, ob, kvb, ct, st,
         pc_sem, rs, rr, zs, zr, xs, xr, ns, nr, shl, shs, shr,
         tl, tas, tar, ts, tr, tfs, tfr, osm, orm, kvs):
    rows = pieces.shape[1]
    cw = pieces.shape[2] // NC
    gw = pieces.shape[2] // NG
    per = NC // NG
    tok_rows, width = tokens.shape
    layers = oldsec.shape[0]
    s = lax.axis_index("section")
    m = lax.axis_index("fsdp")
    y = s // 2
    c = s % 2
    j = m // 16
    x = (m // 4) % 4
    z = m % 4
    h = z % 2
    zh = z // 2
    prob = (j + zh) % 2
    is_a = c == prob
    is_b = c != prob
    alone = jnp.logical_and(c == j, zh == 0)
    not_alone = jnp.logical_or(c != j, zh != 0)

    def dev(yy, cc, jj, xx, zz):
        return (2 * yy + cc, jj * 16 + xx * 4 + zz)

    core_dev = dev(y, 1 - c, j, x, z)
    cross_dev = [dev(1 - y, k, 1 - j, x, z) for k in range(2)]
    zf = (z + 2) % 4
    xp, xm, xf = (x + 1) % 4, (x + 3) % 4, (x + 2) % 4
    xp_dev, xm_dev = (dev(y, c, j, xx, z) for xx in (xp, xm))

    def remote(src, dst, send, recv, device):
        return pltpu.make_async_remote_copy(
            src_ref=src, dst_ref=dst, send_sem=send, recv_sem=recv,
            device_id=device, device_id_type=MESH)

    def arrived(dst, send, recv, device):
        remote(dst, dst, send, recv, device).wait_recv()

    def pc_copy(i, a):
        to = px.at[x, a] if i == 0 else pc.at[i, a]
        return pltpu.make_async_copy(pieces.at[a, :, pl.ds(i * cw, cw)], to, pc_sem.at[i, a])

    for i in range(NC):
        for a in range(2):
            pc_copy(i, a).start()

    def layer_of(section):
        found = jnp.int32(0)
        for l in range(layers):
            found = found + jnp.where(newsec[l] == section, l, 0)
        return found

    def entry(table, layer):
        found = jnp.int32(0)
        for l in range(layers):
            found = found + jnp.where(layer == l, table(l), 0)
        return found

    high = jnp.int32(0)
    for l in range(layers):
        high = jnp.where(oldsec[l] == s, l, high)
    row_high = entry(lambda l: newsec[l], high) // 2
    source = [entry(lambda l: oldsec[l], layer_of(2 * s + k)) for k in range(2)]
    gl = layer_of(2 * (2 * y + prob) + h)
    gl_crossed = jnp.where(entry(lambda l: oldsec[l], gl) // 2 == y, 0, 1)
    gl_old = entry(lambda l: oldord[0, l], gl)
    gl_new = entry(lambda l: neword[0, l], gl)
    gl_turn = (jnp.where(gl_old == gl_new, 0, 1) + gl_crossed + j + c) % 2
    is_key = gl_old == (c + gl_crossed) % 2
    ol = layer_of(2 * s + h)
    ol_crossed = jnp.where(entry(lambda l: oldsec[l], ol) // 2 == y, 0, 1)
    key_at = (entry(lambda l: oldord[0, l], ol) + ol_crossed) % 2

    barrier = pltpu.get_barrier_semaphore()
    partners = cross_dev + [xp_dev, xm_dev]
    for n in range(1, 16):
        partners.append(dev(y, (c + n) % 2, (j + n // 2) % 2, x, (z + n // 4) % 4))
    for device in partners:
        pl.semaphore_signal(barrier, inc=1, device_id=device, device_id_type=MESH)
    pl.semaphore_wait(barrier, len(partners))

    tok_step = width // (2 * TU)
    quarter = width // 4

    slots = [x, xm, xp, xf]

    def tok_cols(u, a):
        start = slots[u // 2] * quarter + (2 * a + u % 2) * tok_step
        return pl.ds(pl.multiple_of(start, tok_step), tok_step)

    def tok_send(v):
        u, a = v // 2, v % 2
        cols = tok_cols(u, a)
        parts = [(pl.ds(0, SPLIT), dev(y, a, 1 - j, x, z)),
                 (pl.ds(SPLIT, tok_rows - SPLIT), dev(y, a, j, x, zf))]
        return [remote(tokens.at[part, cols], xb.at[1, part, cols], ts.at[v, k], tr.at[u, k], device)
                for k, (part, device) in enumerate(parts)]

    def tok_here(u):
        cols = tok_cols(u, c)
        for k, part in enumerate((pl.ds(0, SPLIT), pl.ds(SPLIT, tok_rows - SPLIT))):
            arrived(xb.at[1, part, cols], tfs.at[u], tr.at[u, k], core_dev)

    def tok_pass(u):
        cols = tok_cols(u, c)
        return remote(xb.at[1, :, cols], xb.at[1, :, cols], tfs.at[u], tfr.at[u], core_dev)

    def tok_other(u):
        cols = tok_cols(u, 1 - c)
        return remote(xb.at[1, :, cols], xb.at[1, :, cols], tfs.at[u], tfr.at[u], core_dev)

    def tok_core(k):
        cols = pl.ds(k * quarter, quarter)
        return remote(tokens.at[:, cols], xb.at[0, :, cols], tas.at[k], tar.at[k], core_dev)

    tok_local = pltpu.make_async_copy(tokens, xb.at[0], tl.at[0])
    tok_next = [0]

    def send_tokens(count):
        take = range(tok_next[0], min(tok_next[0] + count, 2 * TU))
        tok_next[0] += len(take)

        @pl.when(is_b)
        def _():
            for v in take:
                for copy in tok_send(v):
                    copy.start()

    def relay_copies(e):
        return [remote(og.at[e, k], cand.at[e, s], rs.at[e, k],
                       rr.at[e, 0] if k == 0 else rr.at[e, 1 + c], device)
                for k, device in enumerate([core_dev] + cross_dev)]

    relay_rows = [2 * y + 1 - c, 2 * (1 - y), 2 * (1 - y) + 1]
    first_entries = [0] + [NC + k for k in range(3)]

    def relay(e, of):
        def tile(t, carry):
            part = pl.ds(pl.multiple_of(t * 128, 128), 128)
            low_rows, high_rows = of(0, part), of(1, part)
            for k in range(3):
                og[e, k, part, :] = jnp.where(row_high == relay_rows[k], high_rows, low_rows)
            cand[e, s, part, :] = jnp.where(row_high == s, high_rows, low_rows)
            return carry

        lax.fori_loop(0, rows // 128, tile, 0)
        for copy in relay_copies(e):
            copy.start()

    def relay_send(i):
        for a in range(2):
            pc_copy(i, a).wait()
        relay(i, lambda a, part: pc[i, a, part, :])

    def relay_first(b):
        relay(first_entries[b], lambda a, part: px[slots[b], a, part, :])

    def place(slot, zz):
        return pl.ds(pl.multiple_of((slots[slot] * 4 + zz) * rows, rows), rows)

    def spread(i, slot):
        copies = []
        for k in range(2):
            src = gb.at[slots[slot], k] if i == 0 else pc.at[i, k]
            target = 2 * ((c + j) % 2) + k
            for far in (1, 0):
                device = dev(y, j, (j + far) % 2, x, (target + 2 * far) % 4)
                copy = remote(src, wb.at[i, place(slot, z)], zs.at[i, slot, 2 * k + far],
                              zr.at[i, slot, z], device)
                here = jnp.logical_and(alone, h == k)
                copies.append((copy, None if far else jnp.logical_not(here)))
        return copies

    def spread_each(i, slot, act):
        for copy, needed in spread(i, slot):
            if needed is None:
                act(copy)
            else:
                @pl.when(needed)
                def _():
                    act(copy)

    def spread_start(i, slot):
        spread_each(i, slot, lambda copy: copy.start())

    def spread_arrived(i, slot):
        for n in range(1, 4):
            zz = (z + n) % 4
            arrived(wb.at[i, place(slot, zz)], zs.at[i, slot, 0], zr.at[i, slot, zz], core_dev)

        @pl.when(not_alone)
        def _():
            arrived(wb.at[i, place(slot, z)], zs.at[i, slot, 0], zr.at[i, slot, z], core_dev)

    def choose_from(e, i, slot, to):
        arrived(cand.at[e, 2 * y + 1 - c], rs.at[e, 0], rr.at[e, 0], core_dev)
        for k in range(2):
            arrived(cand.at[e, 2 * (1 - y) + k], rs.at[e, 1 + k], rr.at[e, 1 + k], cross_dev[k])

        def tile(t, carry):
            part = pl.ds(pl.multiple_of(t * 128, 128), 128)
            four = [cand[e, k, part, :] for k in range(4)]
            for k in range(2):
                want = source[k]
                to[k, part, :] = jnp.where(want < 2, jnp.where(want == 0, four[0], four[1]),
                                           jnp.where(want == 2, four[2], four[3]))
            return carry

        lax.fori_loop(0, rows // 128, tile, 0)
        spread_start(i, slot)

        @pl.when(alone)
        def _():
            def keep(t, carry):
                part = pl.ds(pl.multiple_of(t * 128, 128), 128)
                here = pl.ds(pl.multiple_of((slots[slot] * 4 + z) * rows + t * 128, 128), 128)
                wb[i, here, :] = to[h, part, :]
                return carry

            lax.fori_loop(0, rows // 128, keep, 0)

    def choose(i):
        choose_from(i, i, 0, pc.at[i])

    def choose_first(b):
        choose_from(first_entries[b], 0, b, gb.at[slots[b]])

    def first_own_copies():
        mine = px.at[x]
        return [remote(mine, mine, xs.at[0, 0], xr.at[0, 0], xp_dev),
                remote(mine, mine, xs.at[0, 1], xr.at[0, 1], xm_dev)]

    def first_pass_copies():
        left, right = px.at[xm, 0], px.at[xp, 1]
        return [remote(left, left, xs.at[0, 2], xr.at[0, 2], xp_dev),
                remote(right, right, xs.at[0, 3], xr.at[0, 3], xm_dev)]

    def first_own():
        for a in range(2):
            pc_copy(0, a).wait()
        for copy in first_own_copies():
            copy.start()

    def first_pass():
        arrived(px.at[xm], xs.at[0, 0], xr.at[0, 0], xp_dev)
        arrived(px.at[xp], xs.at[0, 1], xr.at[0, 1], xm_dev)
        for copy in first_pass_copies():
            copy.start()

    def first_far():
        arrived(px.at[xf, 0], xs.at[0, 2], xr.at[0, 2], xp_dev)
        arrived(px.at[xf, 1], xs.at[0, 3], xr.at[0, 3], xm_dev)

    def block(i, xx, first, count):
        return wb.at[i, pl.ds(pl.multiple_of(xx * 4 * rows + first, rows), count)]

    def own_copies(i):
        mine = block(i, x, 0, 4 * rows)
        return [remote(mine, mine, xs.at[i, 0], xr.at[i, 0], xp_dev),
                remote(mine, mine, xs.at[i, 1], xr.at[i, 1], xm_dev)]

    def pass_copies(i):
        left = block(i, xm, 0, 2 * rows)
        right = block(i, xp, 2 * rows, 2 * rows)
        return [remote(left, left, xs.at[i, 2], xr.at[i, 2], xp_dev),
                remote(right, right, xs.at[i, 3], xr.at[i, 3], xm_dev)]

    pair = pl.ds(pl.multiple_of((x * 4 + z // 2 * 2) * rows, rows), 2 * rows)

    def near_copy(i):
        return remote(wb.at[i, pair], n2.at[i], ns.at[i], nr.at[i], core_dev)

    def x_own(i):
        spread_arrived(i, 0)
        if i > 0:
            for copy in own_copies(i):
                copy.start()

        @pl.when(is_b)
        def _():
            near_copy(i).start()

    def x_pass(i):
        arrived(block(i, xm, 0, 4 * rows), xs.at[i, 0], xr.at[i, 0], xp_dev)
        first, second = pass_copies(i)
        first.start()
        arrived(block(i, xp, 0, 4 * rows), xs.at[i, 1], xr.at[i, 1], xm_dev)
        second.start()

    def far_arrived(i):
        if i == 0:
            for slot in (1, 2, 3):
                spread_arrived(i, slot)
            return
        arrived(block(i, xf, 0, 2 * rows), xs.at[i, 2], xr.at[i, 2], xp_dev)
        arrived(block(i, xf, 2 * rows, 2 * rows), xs.at[i, 3], xr.at[i, 3], xm_dev)

    def shard_local(i):
        return pltpu.make_async_copy(sha.at[i], shard_out.at[:, pl.ds(i * cw, cw)], shl.at[i])

    def shard_far(i):
        return remote(shb.at[i], shard_out.at[:, pl.ds(i * cw, cw)], shs.at[i], shr.at[i],
                      dev(y, c, 1 - j, x, z))

    def shard(i):
        @pl.when(is_a)
        def _():
            near_copy(i).wait_recv()

            def tile(t, carry):
                part = pl.ds(pl.multiple_of(t * 128, 128), 128)
                near = pl.ds(pl.multiple_of((x * 4 + z // 2 * 2) * rows + t * 128, 128), 128)
                mine = wb[i, near, :]
                other = n2[i, part, :]
                sha[i, part, :] = jnp.where(gl_turn == 0, mine, other)
                shb[i, part, :] = jnp.where(gl_turn == 0, other, mine)
                return carry

            lax.fori_loop(0, 2 * rows // 128, tile, 0)

    def shard_send(i):
        @pl.when(is_a)
        def _():
            shard_local(i).start()
            shard_far(i).start()

    def multiply(g, slots_now, xx, half):
        first = pl.multiple_of(xx * 4 * rows + half * 2 * rows, 2 * rows)
        ks = pl.ds(first, 2 * rows)
        weight = jnp.concatenate([wb[per * g + k, ks, :] for k in range(per)], axis=1)
        for slot in slots_now:
            acc[g, slot] += jnp.dot(xb[slot, :, ks], weight, preferred_element_type=jnp.float32)

    def clear(g):
        acc[g] = jnp.zeros(acc.shape[1:], acc.dtype)

    def near(g, slots_now, start, stop):
        def near_block(t, carry):
            b = t // 2
            multiply(g, slots_now, (x + 3 * b - b // 2 * 5) % 4, t % 2)
            return carry

        lax.fori_loop(2 * start, 2 * stop, near_block, 0)

    def far(g, slots_now):
        def far_block(t, carry):
            multiply(g, slots_now, xf, t)
            return carry

        lax.fori_loop(0, 2, far_block, 0)

    def finish(g, slot):
        def tile(t, carry):
            part = pl.ds(pl.multiple_of(t * 128, 128), 128)
            cosine = ct[slot, part, :]
            sine = st[slot, part, :]
            for head in range(gw // HEAD_DIM):
                cols = slice(head * HEAD_DIM, (head + 1) * HEAD_DIM)
                value = acc[g, slot, part, cols]
                turned = value * cosine + pltpu.roll(value, HEAD_DIM // 2, 1) * sine
                ob[g, slot, part, cols] = turned.astype(jnp.bfloat16)
            return carry

        lax.fori_loop(0, tok_rows // 128, tile, 0)

    def kv_part(g, q, part):
        return kvb.at[q, part, pl.ds(g * gw, gw)]

    all_rows = pl.ds(0, tok_rows)
    y_rows, z_rows = pl.ds(0, SPLIT), pl.ds(SPLIT, tok_rows - SPLIT)

    def out_near(g):
        return remote(ob.at[g, 0], kv_part(g, c, all_rows), osm.at[g, 0], orm.at[g, c], core_dev)

    def out_far(g):
        return [remote(ob.at[g, 1, y_rows], kv_part(g, c, y_rows), osm.at[g, 1], orm.at[g, c],
                       dev(y, prob, 1 - j, x, z)),
                remote(ob.at[g, 1, z_rows], kv_part(g, c, z_rows), osm.at[g, 2], orm.at[g, 2 + c],
                       dev(y, prob, j, x, zf))]

    def send_far(g):
        for copy in out_far(g):
            copy.start()

    def send_near(g):
        @pl.when(is_a)
        def _():
            def tile(t, carry):
                part = pl.ds(pl.multiple_of(t * 128, 128), 128)
                kvb[c, part, g * gw:(g + 1) * gw] = ob[g, 0, part, :]
                return carry

            lax.fori_loop(0, tok_rows // 128, tile, 0)

        @pl.when(is_b)
        def _():
            out_near(g).start()

    def stage(n):
        return cand.at[1 + n // 4, n % 4]

    def kv_copies(g):
        copies = []
        for n in range(2 * per):
            k, part = n // per, n % per
            cols = pl.ds(k * NG * gw + g * gw + part * cw, cw)
            copies.append(pltpu.make_async_copy(stage(2 * per * g + n), kv_out.at[:, cols],
                                                kvs.at[g, n]))
        return copies

    def collect(g):
        @pl.when(is_a)
        def _():
            arrived(kv_part(g, 1 - c, all_rows), osm.at[g, 0], orm.at[g, 1 - c], core_dev)

        @pl.when(is_b)
        def _():
            for q in range(2):
                arrived(kv_part(g, q, y_rows), osm.at[g, 0], orm.at[g, q], core_dev)
                arrived(kv_part(g, q, z_rows), osm.at[g, 0], orm.at[g, 2 + q], core_dev)

        def tile(t, carry):
            rows_now = pl.ds(pl.multiple_of(t * 128, 128), 128)
            for part in range(per):
                cols = slice(g * gw + part * cw, g * gw + (part + 1) * cw)
                first, second = kvb[0, rows_now, cols], kvb[1, rows_now, cols]
                stage(2 * per * g + part)[rows_now, :] = jnp.where(key_at == 0, first, second)
                stage(2 * per * g + per + part)[rows_now, :] = jnp.where(key_at == 0, second, first)
            return carry

        lax.fori_loop(0, tok_rows // 128, tile, 0)
        for copy in kv_copies(g):
            copy.start()

    def tables():
        first = m // 2 * tok_rows
        by_y = (m // 2 + 8) % 16 * tok_rows
        by_z = (m // 2 + 1 - 2 * zh) * tok_rows
        lane = lax.broadcasted_iota(jnp.int32, (64, HEAD_DIM), 1)
        row = lax.broadcasted_iota(jnp.int32, (64, HEAD_DIM), 0)

        def tile(t, carry):
            part = pl.ds(pl.multiple_of(t * 64, 64), 64)
            for slot in range(2):
                base = first if slot == 0 else jnp.where(t * 64 < SPLIT, by_y, by_z)
                position = (base + t * 64 + row).astype(jnp.float32)
                angle = position * freq[0:1, :]
                sine = jnp.sin(angle)
                sine = jnp.where(lane < HEAD_DIM // 2, -sine, sine)
                ct[slot, part, :] = jnp.where(is_key, jnp.cos(angle), 1.0)
                st[slot, part, :] = jnp.where(is_key, sine, 0.0)
            return carry

        lax.fori_loop(0, tok_rows // 64, tile, 0)

    def token_pass(u):
        tok_here(u)
        tok_pass(u).start()

    def token_other(b):
        for u in (2 * b, 2 * b + 1):
            tok_other(u).wait_recv()

    first_own()
    for i in range(1, NC):
        relay_send(i)
    send_tokens(1)
    choose(1)
    first_pass()
    choose(2)
    x_own(1)
    first_far()
    for b in range(4):
        relay_first(b)
    choose(3)
    x_own(2)

    @pl.when(is_a)
    def _():
        tok_local.start()
        for k in range(4):
            tok_core(k).start()

    choose(4)
    x_own(3)
    x_pass(1)
    choose(5)
    x_own(4)
    choose(6)
    x_own(5)
    choose(7)
    send_tokens(2 * TU)
    x_own(6)
    x_pass(2)
    x_own(7)
    tables()

    @pl.when(is_a)
    def _():
        tok_local.wait()

    @pl.when(is_b)
    def _():
        for k in range(4):
            tok_core(k).wait_recv()

    for g in range(NG):
        clear(g)
    x_pass(3)
    for b in range(4):
        choose_first(b)
    near(1, (0,), 0, 3)
    token_pass(0)
    x_pass(4)
    token_pass(1)
    token_pass(2)
    token_other(0)
    near(1, (1,), 0, 1)
    x_pass(5)
    token_pass(3)
    near(2, (0,), 0, 3)
    token_pass(4)
    x_pass(6)
    token_other(1)
    near(1, (1,), 1, 2)
    near(2, (1,), 0, 2)
    token_pass(5)
    x_pass(7)
    for i in range(1, 5):
        shard(i)
        shard_send(i)
    for i in range(5, 8):
        shard(i)
        shard_send(i)
    near(3, (0,), 0, 3)
    token_pass(6)
    token_other(2)
    for g in (1, 2):
        near(g, (1,), 2, 3)
    near(3, (1,), 0, 3)
    token_pass(7)
    token_other(3)
    x_own(0)
    for g in (1, 2, 0, 3):
        for k in range(per):
            far_arrived(per * g + k)
        if g == 0:
            shard(0)
            shard_send(0)
            near(g, (0, 1), 0, 3)
        if g == 3:
            far(g, (1,))
            finish(g, 1)
            send_far(g)
            far(g, (0,))
            finish(g, 0)
            send_near(g)
        else:
            far(g, (0, 1))
            finish(g, 1)
            send_far(g)
            finish(g, 0)
            send_near(g)
        if g == 0:
            collect(1)
    for g in (2, 0, 3):
        collect(g)

    for e in list(range(NC)) + first_entries[1:]:
        for copy in relay_copies(e):
            copy.wait_send()
    for i in range(NC):
        for copy in first_own_copies() + first_pass_copies() if i == 0 else own_copies(i) + pass_copies(i):
            copy.wait_send()
        for slot in range(4 if i == 0 else 1):
            spread_each(i, slot, lambda copy: copy.wait_send())

    @pl.when(is_a)
    def _():
        for k in range(4):
            tok_core(k).wait_send()
        for i in range(NC):
            shard_local(i).wait()
            shard_far(i).wait_send()

    @pl.when(is_b)
    def _():
        for v in range(2 * TU):
            for copy in tok_send(v):
                copy.wait_send()
        for i in range(NC):
            near_copy(i).wait_send()
            shard_far(i).wait_recv()
        for g in range(NG):
            out_near(g).wait_send()

    for u in range(TU):
        tok_pass(u).wait_send()
    for g in range(NG):
        for copy in out_far(g):
            copy.wait_send()
        for copy in kv_copies(g):
            copy.wait()


def per_device(old_pieces, section_inputs, old_section_of, new_section_of, old_order, new_order):
    pieces = old_pieces[0]
    tokens = section_inputs[0]
    _, rows, kv_width = pieces.shape
    tok_rows, width = tokens.shape
    cw, gw = kv_width // NC, kv_width // NG

    half_dim = HEAD_DIM // 2
    freq_index = (jnp.arange(HEAD_DIM, dtype=jnp.int32) % half_dim).astype(jnp.float32)
    inverse_freq = jnp.exp(freq_index * (-2.0 * math.log(500000.0) / HEAD_DIM))
    freq = jnp.broadcast_to(inverse_freq[None, :], (8, HEAD_DIM))

    dma = pltpu.SemaphoreType.DMA
    bf, fl = jnp.bfloat16, jnp.float32
    hbm = pl.BlockSpec(memory_space=pltpu.HBM)
    vmem = pl.BlockSpec(memory_space=pltpu.VMEM)
    smem = pl.BlockSpec(memory_space=pltpu.SMEM)
    kv, shards = pl.pallas_call(
        body,
        out_shape=(jax.ShapeDtypeStruct((tok_rows, 2 * kv_width), bf),
                   jax.ShapeDtypeStruct((2 * rows, kv_width), bf)),
        in_specs=[smem] * 4 + [vmem] + [hbm] * 2,
        out_specs=(hbm, hbm),
        scratch_shapes=[
            pltpu.VMEM((4, 2, rows, cw), bf),
            pltpu.VMEM((NC, 2, rows, cw), bf),
            pltpu.VMEM((NC + 3, 3, rows, cw), bf),
            pltpu.VMEM((NC + 3, 4, rows, cw), bf),
            pltpu.VMEM((4, 2, rows, cw), bf),
            pltpu.VMEM((NC, width, cw), bf),
            pltpu.VMEM((NC, 2 * rows, cw), bf),
            pltpu.VMEM((NC, 2 * rows, cw), bf),
            pltpu.VMEM((NC, 2 * rows, cw), bf),
            pltpu.VMEM((2, tok_rows, width), bf),
            pltpu.VMEM((NG, 2, tok_rows, gw), fl),
            pltpu.VMEM((NG, 2, tok_rows, gw), bf),
            pltpu.VMEM((2, tok_rows, kv_width), bf),
            pltpu.VMEM((2, tok_rows, HEAD_DIM), fl),
            pltpu.VMEM((2, tok_rows, HEAD_DIM), fl),
            dma((NC, 2)), dma((NC + 3, 3)), dma((NC + 3, 3)),
            dma((NC, 4, 4)), dma((NC, 4, 4)), dma((NC, 4)), dma((NC, 4)),
            dma((NC,)), dma((NC,)), dma((NC,)), dma((NC,)), dma((NC,)),
            dma((1,)), dma((4,)), dma((4,)), dma((2 * TU, 2)), dma((TU, 2)), dma((TU,)), dma((TU,)),
            dma((NG, 3)), dma((NG, 4)), dma((NG, 2 * NC // NG)),
        ],
        compiler_params=pltpu.CompilerParams(
            collective_id=0, has_side_effects=True, vmem_limit_bytes=66_000_000),
    )(old_section_of, new_section_of, old_order.T, new_order.T, freq, pieces, tokens)

    return shards[None], kv[None]


def solution(mesh):
    in_specs = (P("section", None, "fsdp", None), P("section", "fsdp", None), P(), P(), P(), P())
    out_specs = (P("section", "fsdp", None), P("section", "fsdp", None))
    return jax.shard_map(
        per_device, mesh=mesh, in_specs=in_specs, out_specs=out_specs, check_vma=False
    )
```

time: 175 us -> 163 us (0.931)
  Pallas kernels: 166 us -> 157 us
  other arithmetic: 2.12 us -> 0.01 us
    pallas_call x1, Pallas kernels: 166 us -> 157 us  [per_device(): pl.pallas_call(body, out_shape=(jax.ShapeDtypeStruct((tok_rows, 2 * kv_wi...]
    unnamed x3 -> x4, local copies, waits for them, and re-layouts: 1.32 us -> 4.55 us
    slice x2 -> x0, local copies, waits for them, and re-layouts: 2.91 us -> none  [the longest x1 1.71 us: per_device(): kv[1]]
    select_n x1 -> x0, other arithmetic: 2.11 us -> none  [per_device(): jnp.where(swapped, jnp.concatenate([kv[1], kv[0]], axis=-1), jnp.concaten...]
where the time goes in v4:
time: 163 us
  Pallas kernels  157 us (96%)
  local copies, waits for them, and re-layouts  5.15 us (3%)
    pallas_call x1, Pallas kernels, per_device(): pl.pallas_call(body, out_shape=(jax.ShapeDtypeStruct((tok_rows, 2 * kv_wi...  157 us
    unnamed x4, local copies, waits for them, and re-layouts  4.55 us

profile of v4, /device:TPU:1, one launch (start us, length us, event | category | flops | bytes accessed | tf_op | source)
XLA Modules:
  0.0 162.7 jit_solution(10429189179367203957)
XLA Ops:
  0.6 0.6 broadcast_in_dim.12.freq
  1.2 156.9 %shard_map.77 = (bf16[512,2048]{1,0:T(8,128)(2,1)}, bf16[1024,1024]{1,0:T(8,128)(2,1)}) custom-call(s32[8]{0:T(128)} %oldsec.1, s32[8]{0:T(128)} %newsec.1, s32[2,8]{1,0:T(2,128)} %bitcast.10, s32[2,8]{1,0:T(2,128)} %bitcast.11, f32[8,128]{1,0:T(8,128)} %broadcast_in_dim.12.freq, bf16[2,512,1024]{2,1,0:T(8,128)(2,1)} %bitcast.9, bf16[512,8192]{1,0:T(8,128)(2,1)} %bitcast.6), custom_call_target="tpu_custom_call" | custom-call | tf_op jit(solution)/shard_map/pallas_call | solution.py:644
  158.1 0.0 copy-start
  158.2 3.2 %copy.10 = bf16[1,1024,1024]{2,1,0:T(8,128)(2,1)} copy(bf16[1,1024,1024]{2,1,0:T(8,128)(2,1)} %bitcast.8) | data formatting | bytes 4194304
  161.4 0.0 copy-done
  161.4 1.3 copy.11
  (1 shorter events, 0.0 us)
Async XLA Ops:
  158.1 3.2 %copy-start = (bf16[512,2048]{1,0:T(8,128)(2,1)S(1)}, bf16[512,2048]{1,0:T(8,128)(2,1)}, u32[]{:S(2)}) copy-start(bf16[512,2048]{1,0:T(8,128)(2,1)} %get-tuple-element.5) | copy-start | bytes 6291460

commit v5 on v4

--- a/solution.py
+++ b/solution.py
@@ -12,13 +12,13 @@
 NC = 8
 NG = 4
 TU = 8
-SPLIT = 192
+SPLIT = 224
 
 
 def body(oldsec, newsec, oldord, neword, freq, pieces, tokens, kv_out, shard_out,
          px, pc, og, cand, gb, wb, n2, sha, shb, xb, acc, ob, kvb, ct, st,
          pc_sem, rs, rr, zs, zr, xs, xr, ns, nr, shl, shs, shr,
-         tl, tas, tar, ts, tr, tfs, tfr, osm, orm, kvs):
+         tl, tas, tar, ts, tr, tfs, tfr, osm, orm, kvs, xs1, xr1):
     rows = pieces.shape[1]
     cw = pieces.shape[2] // NC
     gw = pieces.shape[2] // NG
@@ -301,11 +301,39 @@
         def _():
             near_copy(i).start()
 
+    def own_pieces(zz):
+        mine = wb.at[1, place(0, zz)]
+        return [remote(mine, mine, xs1.at[0, zz], xr1.at[0, zz], xp_dev),
+                remote(mine, mine, xs1.at[1, zz], xr1.at[1, zz], xm_dev)]
+
+    def x_arrived(i, side, slot, device):
+        if i == 1:
+            for zz in range(4):
+                arrived(wb.at[1, place(slot, zz)], xs1.at[side, zz], xr1.at[side, zz], device)
+        else:
+            arrived(block(i, slots[slot], 0, 4 * rows), xs.at[i, side], xr.at[i, side], device)
+
+    def x_own_first():
+        for n in (0, 1, 3, 2):
+            zz = (z + n) % 4
+            if n == 0:
+                @pl.when(not_alone)
+                def _():
+                    arrived(wb.at[1, place(0, z)], zs.at[1, 0, 0], zr.at[1, 0, z], core_dev)
+            else:
+                arrived(wb.at[1, place(0, zz)], zs.at[1, 0, 0], zr.at[1, 0, zz], core_dev)
+            for copy in own_pieces(zz):
+                copy.start()
+
+        @pl.when(is_b)
+        def _():
+            near_copy(1).start()
+
     def x_pass(i):
-        arrived(block(i, xm, 0, 4 * rows), xs.at[i, 0], xr.at[i, 0], xp_dev)
+        x_arrived(i, 0, 1, xp_dev)
         first, second = pass_copies(i)
         first.start()
-        arrived(block(i, xp, 0, 4 * rows), xs.at[i, 1], xr.at[i, 1], xm_dev)
+        x_arrived(i, 1, 2, xm_dev)
         second.start()
 
     def far_arrived(i):
@@ -463,7 +491,7 @@
         def tile(t, carry):
             part = pl.ds(pl.multiple_of(t * 64, 64), 64)
             for slot in range(2):
-                base = first if slot == 0 else jnp.where(t * 64 < SPLIT, by_y, by_z)
+                base = first if slot == 0 else jnp.where(t * 64 + row < SPLIT, by_y, by_z)
                 position = (base + t * 64 + row).astype(jnp.float32)
                 angle = position * freq[0:1, :]
                 sine = jnp.sin(angle)
@@ -482,6 +510,13 @@
         for u in (2 * b, 2 * b + 1):
             tok_other(u).wait_recv()
 
+    def sent_copies(i):
+        if i == 0:
+            return first_own_copies() + first_pass_copies()
+        if i == 1:
+            return sum([own_pieces(zz) for zz in range(4)], pass_copies(1))
+        return own_copies(i) + pass_copies(i)
+
     first_own()
     for i in range(1, NC):
         relay_send(i)
@@ -489,7 +524,7 @@
     choose(1)
     first_pass()
     choose(2)
-    x_own(1)
+    x_own_first()
     first_far()
     for b in range(4):
         relay_first(b)
@@ -510,7 +545,7 @@
     choose(6)
     x_own(5)
     choose(7)
-    send_tokens(2 * TU)
+    send_tokens(TU)
     x_own(6)
     x_pass(2)
     x_own(7)
@@ -530,68 +565,66 @@
     x_pass(3)
     for b in range(4):
         choose_first(b)
+    send_tokens(2 * TU)
     near(1, (0,), 0, 3)
     token_pass(0)
     x_pass(4)
     token_pass(1)
-    token_pass(2)
     token_other(0)
     near(1, (1,), 0, 1)
+    token_pass(2)
+    token_pass(3)
     x_pass(5)
-    token_pass(3)
-    near(2, (0,), 0, 3)
-    token_pass(4)
-    x_pass(6)
     token_other(1)
     near(1, (1,), 1, 2)
+    near(2, (0,), 0, 3)
     near(2, (1,), 0, 2)
-    token_pass(5)
-    x_pass(7)
-    for i in range(1, 5):
+    x_pass(6)
+    for i in range(1, 8):
         shard(i)
         shard_send(i)
-    for i in range(5, 8):
-        shard(i)
-        shard_send(i)
+    x_own(0)
+    far_arrived(0)
+    near(0, (0,), 0, 3)
+    near(0, (1,), 0, 2)
+    x_pass(7)
     near(3, (0,), 0, 3)
+    shard(0)
+    shard_send(0)
+    token_pass(4)
+    token_pass(5)
+    token_other(2)
+    near(0, (1,), 2, 3)
+    near(1, (1,), 2, 3)
+    near(2, (1,), 2, 3)
+    near(3, (1,), 0, 3)
+    far_arrived(1)
+    far(0, (0,))
+    far_arrived(2)
+    far_arrived(3)
+    far(1, (0,))
     token_pass(6)
-    token_other(2)
-    for g in (1, 2):
-        near(g, (1,), 2, 3)
-    near(3, (1,), 0, 3)
     token_pass(7)
     token_other(3)
-    x_own(0)
-    for g in (1, 2, 0, 3):
-        for k in range(per):
-            far_arrived(per * g + k)
-        if g == 0:
-            shard(0)
-            shard_send(0)
-            near(g, (0, 1), 0, 3)
-        if g == 3:
-            far(g, (1,))
-            finish(g, 1)
-            send_far(g)
+    for g in range(NG):
+        if g >= 2:
+            for k in range(per):
+                far_arrived(per * g + k)
+        far(g, (1,))
+        finish(g, 1)
+        send_far(g)
+        if g >= 2:
             far(g, (0,))
-            finish(g, 0)
-            send_near(g)
-        else:
-            far(g, (0, 1))
-            finish(g, 1)
-            send_far(g)
-            finish(g, 0)
-            send_near(g)
-        if g == 0:
-            collect(1)
-    for g in (2, 0, 3):
+        finish(g, 0)
+        send_near(g)
+    for g in range(NG):
         collect(g)
 
     for e in list(range(NC)) + first_entries[1:]:
         for copy in relay_copies(e):
             copy.wait_send()
     for i in range(NC):
-        for copy in first_own_copies() + first_pass_copies() if i == 0 else own_copies(i) + pass_copies(i):
+        for copy in sent_copies(i):
             copy.wait_send()
         for slot in range(4 if i == 0 else 1):
             spread_each(i, slot, lambda copy: copy.wait_send())
@@ -668,6 +701,7 @@
             dma((NC,)), dma((NC,)), dma((NC,)), dma((NC,)), dma((NC,)),
             dma((1,)), dma((4,)), dma((4,)), dma((2 * TU, 2)), dma((TU, 2)), dma((TU,)), dma((TU,)),
             dma((NG, 3)), dma((NG, 4)), dma((NG, 2 * NC // NG)),
+            dma((2, 4)), dma((2, 4)),
         ],
         compiler_params=pltpu.CompilerParams(
             collective_id=0, has_side_effects=True, vmem_limit_bytes=66_000_000),

time: 163 us -> 161 us (0.988)
  Pallas kernels: 157 us -> 155 us
    pallas_call x1, Pallas kernels: 157 us -> 155 us  [per_device(): pl.pallas_call(body, out_shape=(jax.ShapeDtypeStruct((tok_rows, 2 * kv_wi...]
where the time goes in v5:
time: 161 us
  Pallas kernels  155 us (96%)
  local copies, waits for them, and re-layouts  5.15 us (3%)
    pallas_call x1, Pallas kernels, per_device(): pl.pallas_call(body, out_shape=(jax.ShapeDtypeStruct((tok_rows, 2 * kv_wi...  155 us
    unnamed x4, local copies, waits for them, and re-layouts  4.55 us

profile of v5, /device:TPU:1, one launch (start us, length us, event | category | flops | bytes accessed | tf_op | source)
XLA Modules:
  0.0 160.6 jit_solution(14337662001010284446)
XLA Ops:
  0.6 0.6 broadcast_in_dim.12.freq
  1.2 154.8 %shard_map.77 = (bf16[512,2048]{1,0:T(8,128)(2,1)}, bf16[1024,1024]{1,0:T(8,128)(2,1)}) custom-call(s32[8]{0:T(128)} %oldsec.1, s32[8]{0:T(128)} %newsec.1, s32[2,8]{1,0:T(2,128)} %bitcast.10, s32[2,8]{1,0:T(2,128)} %bitcast.11, f32[8,128]{1,0:T(8,128)} %broadcast_in_dim.12.freq, bf16[2,512,1024]{2,1,0:T(8,128)(2,1)} %bitcast.9, bf16[512,8192]{1,0:T(8,128)(2,1)} %bitcast.6), custom_call_target="tpu_custom_call" | custom-call | tf_op jit(solution)/shard_map/pallas_call | solution.py:677
  156.1 0.0 copy-start
  156.1 3.2 %copy.10 = bf16[1,1024,1024]{2,1,0:T(8,128)(2,1)} copy(bf16[1,1024,1024]{2,1,0:T(8,128)(2,1)} %bitcast.8) | data formatting | bytes 4194304
  159.3 0.0 copy-done
  159.3 1.3 copy.11
  (1 shorter events, 0.0 us)
Async XLA Ops:
  156.1 3.2 %copy-start = (bf16[512,2048]{1,0:T(8,128)(2,1)S(1)}, bf16[512,2048]{1,0:T(8,128)(2,1)}, u32[]{:S(2)}) copy-start(bf16[512,2048]{1,0:T(8,128)(2,1)} %get-tuple-element.5) | copy-start | bytes 6291460

commit v6 on v5

--- a/solution.py
+++ b/solution.py
@@ -18,7 +18,7 @@
 def body(oldsec, newsec, oldord, neword, freq, pieces, tokens, kv_out, shard_out,
          px, pc, og, cand, gb, wb, n2, sha, shb, xb, acc, ob, kvb, ct, st,
          pc_sem, rs, rr, zs, zr, xs, xr, ns, nr, shl, shs, shr,
-         tl, tas, tar, ts, tr, tfs, tfr, osm, orm, kvs, xs1, xr1):
+         tl, tas, tar, ts, tr, tfs, tfr, osm, orm, kvs, xr1):
     rows = pieces.shape[1]
     cw = pieces.shape[2] // NC
     gw = pieces.shape[2] // NG
@@ -57,13 +57,12 @@
     def arrived(dst, send, recv, device):
         remote(dst, dst, send, recv, device).wait_recv()
 
-    def pc_copy(i, a):
-        to = px.at[x, a] if i == 0 else pc.at[i, a]
-        return pltpu.make_async_copy(pieces.at[a, :, pl.ds(i * cw, cw)], to, pc_sem.at[i, a])
+    def pc_copy(i):
+        to = px.at[x] if i == 0 else pc.at[i]
+        return pltpu.make_async_copy(pieces.at[:, :, pl.ds(i * cw, cw)], to, pc_sem.at[i])
 
     for i in range(NC):
-        for a in range(2):
-            pc_copy(i, a).start()
+        pc_copy(i).start()
 
     def layer_of(section):
         found = jnp.int32(0)
@@ -114,25 +113,25 @@
         cols = tok_cols(u, a)
         parts = [(pl.ds(0, SPLIT), dev(y, a, 1 - j, x, z)),
                  (pl.ds(SPLIT, tok_rows - SPLIT), dev(y, a, j, x, zf))]
-        return [remote(tokens.at[part, cols], xb.at[1, part, cols], ts.at[v, k], tr.at[u, k], device)
+        return [remote(tokens.at[part, cols], xb.at[1, part, cols], ts.at[0], tr.at[u, k], device)
                 for k, (part, device) in enumerate(parts)]
 
     def tok_here(u):
         cols = tok_cols(u, c)
         for k, part in enumerate((pl.ds(0, SPLIT), pl.ds(SPLIT, tok_rows - SPLIT))):
-            arrived(xb.at[1, part, cols], tfs.at[u], tr.at[u, k], core_dev)
+            arrived(xb.at[1, part, cols], tfs.at[0], tr.at[u, k], core_dev)
 
     def tok_pass(u):
         cols = tok_cols(u, c)
-        return remote(xb.at[1, :, cols], xb.at[1, :, cols], tfs.at[u], tfr.at[u], core_dev)
+        return remote(xb.at[1, :, cols], xb.at[1, :, cols], tfs.at[0], tfr.at[u], core_dev)
 
     def tok_other(u):
         cols = tok_cols(u, 1 - c)
-        return remote(xb.at[1, :, cols], xb.at[1, :, cols], tfs.at[u], tfr.at[u], core_dev)
+        return remote(xb.at[1, :, cols], xb.at[1, :, cols], tfs.at[0], tfr.at[u], core_dev)
 
     def tok_core(k):
         cols = pl.ds(k * quarter, quarter)
-        return remote(tokens.at[:, cols], xb.at[0, :, cols], tas.at[k], tar.at[k], core_dev)
+        return remote(tokens.at[:, cols], xb.at[0, :, cols], tas.at[0], tar.at[k], core_dev)
 
     tok_local = pltpu.make_async_copy(tokens, xb.at[0], tl.at[0])
     tok_next = [0]
@@ -148,7 +147,7 @@
                     copy.start()
 
     def relay_copies(e):
-        return [remote(og.at[e, k], cand.at[e, s], rs.at[e, k],
+        return [remote(og.at[e, k], cand.at[e, s], rs.at[0],
                        rr.at[e, 0] if k == 0 else rr.at[e, 1 + c], device)
                 for k, device in enumerate([core_dev] + cross_dev)]
 
@@ -169,12 +168,14 @@
             copy.start()
 
     def relay_send(i):
-        for a in range(2):
-            pc_copy(i, a).wait()
+        pc_copy(i).wait()
         relay(i, lambda a, part: pc[i, a, part, :])
 
     def relay_first(b):
         relay(first_entries[b], lambda a, part: px[slots[b], a, part, :])
+
+    def entry_of(i, slot):
+        return first_entries[slot] if i == 0 else i
 
     def place(slot, zz):
         return pl.ds(pl.multiple_of((slots[slot] * 4 + zz) * rows, rows), rows)
@@ -186,8 +187,8 @@
             target = 2 * ((c + j) % 2) + k
             for far in (1, 0):
                 device = dev(y, j, (j + far) % 2, x, (target + 2 * far) % 4)
-                copy = remote(src, wb.at[i, place(slot, z)], zs.at[i, slot, 2 * k + far],
-                              zr.at[i, slot, z], device)
+                copy = remote(src, wb.at[i, place(slot, z)], zs.at[far + 2 * (i == 0)],
+                              zr.at[entry_of(i, slot), z], device)
                 here = jnp.logical_and(alone, h == k)
                 copies.append((copy, None if far else jnp.logical_not(here)))
         return copies
@@ -207,16 +208,16 @@
     def spread_arrived(i, slot):
         for n in range(1, 4):
             zz = (z + n) % 4
-            arrived(wb.at[i, place(slot, zz)], zs.at[i, slot, 0], zr.at[i, slot, zz], core_dev)
+            arrived(wb.at[i, place(slot, zz)], zs.at[0], zr.at[entry_of(i, slot), zz], core_dev)
 
         @pl.when(not_alone)
         def _():
-            arrived(wb.at[i, place(slot, z)], zs.at[i, slot, 0], zr.at[i, slot, z], core_dev)
+            arrived(wb.at[i, place(slot, z)], zs.at[0], zr.at[entry_of(i, slot), z], core_dev)
 
     def choose_from(e, i, slot, to):
-        arrived(cand.at[e, 2 * y + 1 - c], rs.at[e, 0], rr.at[e, 0], core_dev)
+        arrived(cand.at[e, 2 * y + 1 - c], rs.at[0], rr.at[e, 0], core_dev)
         for k in range(2):
-            arrived(cand.at[e, 2 * (1 - y) + k], rs.at[e, 1 + k], rr.at[e, 1 + k], cross_dev[k])
+            arrived(cand.at[e, 2 * (1 - y) + k], rs.at[0], rr.at[e, 1 + k], cross_dev[k])
 
         def tile(t, carry):
             part = pl.ds(pl.multiple_of(t * 128, 128), 128)
@@ -248,48 +249,47 @@
 
     def first_own_copies():
         mine = px.at[x]
-        return [remote(mine, mine, xs.at[0, 0], xr.at[0, 0], xp_dev),
-                remote(mine, mine, xs.at[0, 1], xr.at[0, 1], xm_dev)]
+        return [remote(mine, mine, xs.at[0], xr.at[0, 0], xp_dev),
+                remote(mine, mine, xs.at[0], xr.at[0, 1], xm_dev)]
 
     def first_pass_copies():
         left, right = px.at[xm, 0], px.at[xp, 1]
-        return [remote(left, left, xs.at[0, 2], xr.at[0, 2], xp_dev),
-                remote(right, right, xs.at[0, 3], xr.at[0, 3], xm_dev)]
+        return [remote(left, left, xs.at[0], xr.at[0, 2], xp_dev),
+                remote(right, right, xs.at[0], xr.at[0, 3], xm_dev)]
 
     def first_own():
-        for a in range(2):
-            pc_copy(0, a).wait()
+        pc_copy(0).wait()
         for copy in first_own_copies():
             copy.start()
 
     def first_pass():
-        arrived(px.at[xm], xs.at[0, 0], xr.at[0, 0], xp_dev)
-        arrived(px.at[xp], xs.at[0, 1], xr.at[0, 1], xm_dev)
+        arrived(px.at[xm], xs.at[0], xr.at[0, 0], xp_dev)
+        arrived(px.at[xp], xs.at[0], xr.at[0, 1], xm_dev)
         for copy in first_pass_copies():
             copy.start()
 
     def first_far():
-        arrived(px.at[xf, 0], xs.at[0, 2], xr.at[0, 2], xp_dev)
-        arrived(px.at[xf, 1], xs.at[0, 3], xr.at[0, 3], xm_dev)
+        arrived(px.at[xf, 0], xs.at[0], xr.at[0, 2], xp_dev)
+        arrived(px.at[xf, 1], xs.at[0], xr.at[0, 3], xm_dev)
 
     def block(i, xx, first, count):
         return wb.at[i, pl.ds(pl.multiple_of(xx * 4 * rows + first, rows), count)]
 
     def own_copies(i):
         mine = block(i, x, 0, 4 * rows)
-        return [remote(mine, mine, xs.at[i, 0], xr.at[i, 0], xp_dev),
-                remote(mine, mine, xs.at[i, 1], xr.at[i, 1], xm_dev)]
+        return [remote(mine, mine, xs.at[1], xr.at[i, 0], xp_dev),
+                remote(mine, mine, xs.at[1], xr.at[i, 1], xm_dev)]
 
     def pass_copies(i):
         left = block(i, xm, 0, 2 * rows)
         right = block(i, xp, 2 * rows, 2 * rows)
-        return [remote(left, left, xs.at[i, 2], xr.at[i, 2], xp_dev),
-                remote(right, right, xs.at[i, 3], xr.at[i, 3], xm_dev)]
+        return [remote(left, left, xs.at[1], xr.at[i, 2], xp_dev),
+                remote(right, right, xs.at[1], xr.at[i, 3], xm_dev)]
 
     pair = pl.ds(pl.multiple_of((x * 4 + z // 2 * 2) * rows, rows), 2 * rows)
 
     def near_copy(i):
-        return remote(wb.at[i, pair], n2.at[i], ns.at[i], nr.at[i], core_dev)
+        return remote(wb.at[i, pair], n2.at[i], ns.at[0], nr.at[i], core_dev)
 
     def x_own(i):
         spread_arrived(i, 0)
@@ -303,15 +303,15 @@
 
     def own_pieces(zz):
         mine = wb.at[1, place(0, zz)]
-        return [remote(mine, mine, xs1.at[0, zz], xr1.at[0, zz], xp_dev),
-                remote(mine, mine, xs1.at[1, zz], xr1.at[1, zz], xm_dev)]
+        return [remote(mine, mine, xs.at[1], xr1.at[0, zz], xp_dev),
+                remote(mine, mine, xs.at[1], xr1.at[1, zz], xm_dev)]
 
     def x_arrived(i, side, slot, device):
         if i == 1:
             for zz in range(4):
-                arrived(wb.at[1, place(slot, zz)], xs1.at[side, zz], xr1.at[side, zz], device)
+                arrived(wb.at[1, place(slot, zz)], xs.at[1], xr1.at[side, zz], device)
         else:
-            arrived(block(i, slots[slot], 0, 4 * rows), xs.at[i, side], xr.at[i, side], device)
+            arrived(block(i, slots[slot], 0, 4 * rows), xs.at[1], xr.at[i, side], device)
 
     def x_own_first():
         for n in (0, 1, 3, 2):
@@ -319,9 +319,9 @@
             if n == 0:
                 @pl.when(not_alone)
                 def _():
-                    arrived(wb.at[1, place(0, z)], zs.at[1, 0, 0], zr.at[1, 0, z], core_dev)
+                    arrived(wb.at[1, place(0, z)], zs.at[0], zr.at[1, z], core_dev)
             else:
-                arrived(wb.at[1, place(0, zz)], zs.at[1, 0, 0], zr.at[1, 0, zz], core_dev)
+                arrived(wb.at[1, place(0, zz)], zs.at[0], zr.at[1, zz], core_dev)
             for copy in own_pieces(zz):
                 copy.start()
 
@@ -341,14 +341,14 @@
             for slot in (1, 2, 3):
                 spread_arrived(i, slot)
             return
-        arrived(block(i, xf, 0, 2 * rows), xs.at[i, 2], xr.at[i, 2], xp_dev)
-        arrived(block(i, xf, 2 * rows, 2 * rows), xs.at[i, 3], xr.at[i, 3], xm_dev)
+        arrived(block(i, xf, 0, 2 * rows), xs.at[1], xr.at[i, 2], xp_dev)
+        arrived(block(i, xf, 2 * rows, 2 * rows), xs.at[1], xr.at[i, 3], xm_dev)
 
     def shard_local(i):
         return pltpu.make_async_copy(sha.at[i], shard_out.at[:, pl.ds(i * cw, cw)], shl.at[i])
 
     def shard_far(i):
-        return remote(shb.at[i], shard_out.at[:, pl.ds(i * cw, cw)], shs.at[i], shr.at[i],
+        return remote(shb.at[i], shard_out.at[:, pl.ds(i * cw, cw)], shs.at[0], shr.at[0],
                       dev(y, c, 1 - j, x, z))
 
     def shard(i):
@@ -509,13 +509,6 @@
     def token_other(b):
         for u in (2 * b, 2 * b + 1):
             tok_other(u).wait_recv()
-
-    def sent_copies(i):
-        if i == 0:
-            return first_own_copies() + first_pass_copies()
-        if i == 1:
-            return sum([own_pieces(zz) for zz in range(4)], pass_copies(1))
-        return own_copies(i) + pass_copies(i)
 
     first_own()
     for i in range(1, NC):
@@ -620,36 +613,42 @@
     for g in range(NG):
         collect(g)
 
-    for e in list(range(NC)) + first_entries[1:]:
-        for copy in relay_copies(e):
-            copy.wait_send()
-    for i in range(NC):
-        for copy in sent_copies(i):
-            copy.wait_send()
-        for slot in range(4 if i == 0 else 1):
-            spread_each(i, slot, lambda copy: copy.wait_send())
+    def sent(src, send):
+        remote(src, src, send, nr.at[0], core_dev).wait_send()
+
+    later = pl.ds(1, NC - 1)
+    sent(og, rs.at[0])
+    sent(px.at[pl.ds(0, 3)], xs.at[0])
+    sent(wb.at[later, pl.ds(0, 12 * rows)], xs.at[1])
+    sent(pc.at[later], zs.at[1])
+    sent(gb, zs.at[3])
+
+    @pl.when(not_alone)
+    def _():
+        sent(pc.at[later], zs.at[0])
+        sent(gb, zs.at[2])
+
+    @pl.when(alone)
+    def _():
+        sent(pc.at[later, pl.ds(0, 1)], zs.at[0])
+        sent(gb.at[:, pl.ds(0, 1)], zs.at[2])
 
     @pl.when(is_a)
     def _():
-        for k in range(4):
-            tok_core(k).wait_send()
+        sent(tokens, tas.at[0])
         for i in range(NC):
             shard_local(i).wait()
-            shard_far(i).wait_send()
+        sent(shb, shs.at[0])
 
     @pl.when(is_b)
     def _():
-        for v in range(2 * TU):
-            for copy in tok_send(v):
-                copy.wait_send()
-        for i in range(NC):
-            near_copy(i).wait_send()
-            shard_far(i).wait_recv()
+        sent(tokens, ts.at[0])
+        sent(n2, ns.at[0])
+        arrived(shard_out, shs.at[0], shr.at[0], core_dev)
         for g in range(NG):
             out_near(g).wait_send()
 
-    for u in range(TU):
-        tok_pass(u).wait_send()
+    sent(xb.at[1, :, pl.ds(0, 2 * quarter)], tfs.at[0])
     for g in range(NG):
         for copy in out_far(g):
             copy.wait_send()
@@ -696,12 +695,12 @@
             pltpu.VMEM((2, tok_rows, kv_width), bf),
             pltpu.VMEM((2, tok_rows, HEAD_DIM), fl),
             pltpu.VMEM((2, tok_rows, HEAD_DIM), fl),
-            dma((NC, 2)), dma((NC + 3, 3)), dma((NC + 3, 3)),
-            dma((NC, 4, 4)), dma((NC, 4, 4)), dma((NC, 4)), dma((NC, 4)),
-            dma((NC,)), dma((NC,)), dma((NC,)), dma((NC,)), dma((NC,)),
-            dma((1,)), dma((4,)), dma((4,)), dma((2 * TU, 2)), dma((TU, 2)), dma((TU,)), dma((TU,)),
+            dma((NC,)), dma((1,)), dma((NC + 3, 3)),
+            dma((4,)), dma((NC + 3, 4)), dma((2,)), dma((NC, 4)),
+            dma((1,)), dma((NC,)), dma((NC,)), dma((1,)), dma((1,)),
+            dma((1,)), dma((1,)), dma((4,)), dma((1,)), dma((TU, 2)), dma((1,)), dma((TU,)),
             dma((NG, 3)), dma((NG, 4)), dma((NG, 2 * NC // NG)),
-            dma((2, 4)), dma((2, 4)),
+            dma((2, 4)),
         ],
         compiler_params=pltpu.CompilerParams(
             collective_id=0, has_side_effects=True, vmem_limit_bytes=66_000_000),

time: 161 us -> 158 us (0.981)
  Pallas kernels: 155 us -> 152 us
    pallas_call x1, Pallas kernels: 155 us -> 152 us  [per_device(): pl.pallas_call(body, out_shape=(jax.ShapeDtypeStruct((tok_rows, 2 * kv_wi...]
where the time goes in v6:
time: 158 us
  Pallas kernels  152 us (96%)
  local copies, waits for them, and re-layouts  5.15 us (3%)
    pallas_call x1, Pallas kernels, per_device(): pl.pallas_call(body, out_shape=(jax.ShapeDtypeStruct((tok_rows, 2 * kv_wi...  152 us
    unnamed x4, local copies, waits for them, and re-layouts  4.55 us

profile of v6, /device:TPU:1, one launch (start us, length us, event | category | flops | bytes accessed | tf_op | source)
XLA Modules:
  0.0 157.5 jit_solution(10257673784543029118)
XLA Ops:
  0.6 0.6 broadcast_in_dim.12.freq
  1.2 151.7 %shard_map.77 = (bf16[512,2048]{1,0:T(8,128)(2,1)}, bf16[1024,1024]{1,0:T(8,128)(2,1)}) custom-call(s32[8]{0:T(128)} %oldsec.1, s32[8]{0:T(128)} %newsec.1, s32[2,8]{1,0:T(2,128)} %bitcast.10, s32[2,8]{1,0:T(2,128)} %bitcast.11, f32[8,128]{1,0:T(8,128)} %broadcast_in_dim.12.freq, bf16[2,512,1024]{2,1,0:T(8,128)(2,1)} %bitcast.9, bf16[512,8192]{1,0:T(8,128)(2,1)} %bitcast.6), custom_call_target="tpu_custom_call" | custom-call | tf_op jit(solution)/shard_map/pallas_call | solution.py:676
  152.9 0.0 copy-start
  153.0 3.2 %copy.10 = bf16[1,1024,1024]{2,1,0:T(8,128)(2,1)} copy(bf16[1,1024,1024]{2,1,0:T(8,128)(2,1)} %bitcast.8) | data formatting | bytes 4194304
  156.2 0.0 copy-done
  156.2 1.3 copy.11
  (1 shorter events, 0.0 us)
Async XLA Ops:
  152.9 3.2 %copy-start = (bf16[512,2048]{1,0:T(8,128)(2,1)S(1)}, bf16[512,2048]{1,0:T(8,128)(2,1)}, u32[]{:S(2)}) copy-start(bf16[512,2048]{1,0:T(8,128)(2,1)} %get-tuple-element.5) | copy-start | bytes 6291460

commit v7 on v6

--- a/solution.py
+++ b/solution.py
@@ -113,13 +113,12 @@
         cols = tok_cols(u, a)
         parts = [(pl.ds(0, SPLIT), dev(y, a, 1 - j, x, z)),
                  (pl.ds(SPLIT, tok_rows - SPLIT), dev(y, a, j, x, zf))]
-        return [remote(tokens.at[part, cols], xb.at[1, part, cols], ts.at[0], tr.at[u, k], device)
+        return [remote(tokens.at[part, cols], xb.at[1, part, cols], ts.at[0], tr.at[u], device)
                 for k, (part, device) in enumerate(parts)]
 
     def tok_here(u):
         cols = tok_cols(u, c)
-        for k, part in enumerate((pl.ds(0, SPLIT), pl.ds(SPLIT, tok_rows - SPLIT))):
-            arrived(xb.at[1, part, cols], tfs.at[0], tr.at[u, k], core_dev)
+        arrived(xb.at[1, :, cols], tfs.at[0], tr.at[u], core_dev)
 
     def tok_pass(u):
         cols = tok_cols(u, c)
@@ -148,7 +147,7 @@
 
     def relay_copies(e):
         return [remote(og.at[e, k], cand.at[e, s], rs.at[0],
-                       rr.at[e, 0] if k == 0 else rr.at[e, 1 + c], device)
+                       rr.at[e], device)
                 for k, device in enumerate([core_dev] + cross_dev)]
 
     relay_rows = [2 * y + 1 - c, 2 * (1 - y), 2 * (1 - y) + 1]
@@ -215,9 +214,7 @@
             arrived(wb.at[i, place(slot, z)], zs.at[0], zr.at[entry_of(i, slot), z], core_dev)
 
     def choose_from(e, i, slot, to):
-        arrived(cand.at[e, 2 * y + 1 - c], rs.at[0], rr.at[e, 0], core_dev)
-        for k in range(2):
-            arrived(cand.at[e, 2 * (1 - y) + k], rs.at[0], rr.at[e, 1 + k], cross_dev[k])
+        arrived(og.at[e], rs.at[0], rr.at[e], core_dev)
 
         def tile(t, carry):
             part = pl.ds(pl.multiple_of(t * 128, 128), 128)
@@ -419,12 +416,12 @@
     y_rows, z_rows = pl.ds(0, SPLIT), pl.ds(SPLIT, tok_rows - SPLIT)
 
     def out_near(g):
-        return remote(ob.at[g, 0], kv_part(g, c, all_rows), osm.at[g, 0], orm.at[g, c], core_dev)
+        return remote(ob.at[g, 0], kv_part(g, c, all_rows), osm.at[g, 0], orm.at[g], core_dev)
 
     def out_far(g):
-        return [remote(ob.at[g, 1, y_rows], kv_part(g, c, y_rows), osm.at[g, 1], orm.at[g, c],
+        return [remote(ob.at[g, 1, y_rows], kv_part(g, c, y_rows), osm.at[g, 1], orm.at[g],
                        dev(y, prob, 1 - j, x, z)),
-                remote(ob.at[g, 1, z_rows], kv_part(g, c, z_rows), osm.at[g, 2], orm.at[g, 2 + c],
+                remote(ob.at[g, 1, z_rows], kv_part(g, c, z_rows), osm.at[g, 2], orm.at[g],
                        dev(y, prob, j, x, zf))]
 
     def send_far(g):
@@ -460,13 +457,11 @@
     def collect(g):
         @pl.when(is_a)
         def _():
-            arrived(kv_part(g, 1 - c, all_rows), osm.at[g, 0], orm.at[g, 1 - c], core_dev)
+            arrived(kv_part(g, 1 - c, all_rows), osm.at[g, 0], orm.at[g], core_dev)
 
         @pl.when(is_b)
         def _():
-            for q in range(2):
-                arrived(kv_part(g, q, y_rows), osm.at[g, 0], orm.at[g, q], core_dev)
-                arrived(kv_part(g, q, z_rows), osm.at[g, 0], orm.at[g, 2 + q], core_dev)
+            arrived(kvb.at[:, :, pl.ds(g * gw, gw)], osm.at[g, 0], orm.at[g], core_dev)
 
         def tile(t, carry):
             rows_now = pl.ds(pl.multiple_of(t * 128, 128), 128)
@@ -695,11 +690,11 @@
             pltpu.VMEM((2, tok_rows, kv_width), bf),
             pltpu.VMEM((2, tok_rows, HEAD_DIM), fl),
             pltpu.VMEM((2, tok_rows, HEAD_DIM), fl),
-            dma((NC,)), dma((1,)), dma((NC + 3, 3)),
+            dma((NC,)), dma((1,)), dma((NC + 3,)),
             dma((4,)), dma((NC + 3, 4)), dma((2,)), dma((NC, 4)),
             dma((1,)), dma((NC,)), dma((NC,)), dma((1,)), dma((1,)),
-            dma((1,)), dma((1,)), dma((4,)), dma((1,)), dma((TU, 2)), dma((1,)), dma((TU,)),
-            dma((NG, 3)), dma((NG, 4)), dma((NG, 2 * NC // NG)),
+            dma((1,)), dma((1,)), dma((4,)), dma((1,)), dma((TU,)), dma((1,)), dma((TU,)),
+            dma((NG, 3)), dma((NG,)), dma((NG, 2 * NC // NG)),
             dma((2, 4)),
         ],
         compiler_params=pltpu.CompilerParams(

time: 158 us -> 157 us (level)
  no operation moved by 1% of the time
where the time goes in v7:
time: 157 us
  Pallas kernels  151 us (96%)
  local copies, waits for them, and re-layouts  5.15 us (3%)
    pallas_call x1, Pallas kernels, per_device(): pl.pallas_call(body, out_shape=(jax.ShapeDtypeStruct((tok_rows, 2 * kv_wi...  151 us
    unnamed x4, local copies, waits for them, and re-layouts  4.55 us

profile of v7, /device:TPU:1, one launch (start us, length us, event | category | flops | bytes accessed | tf_op | source)
XLA Modules:
  0.0 157.1 jit_solution(15176693232726259191)
XLA Ops:
  0.6 0.6 broadcast_in_dim.12.freq
  1.2 151.3 %shard_map.77 = (bf16[512,2048]{1,0:T(8,128)(2,1)}, bf16[1024,1024]{1,0:T(8,128)(2,1)}) custom-call(s32[8]{0:T(128)} %oldsec.1, s32[8]{0:T(128)} %newsec.1, s32[2,8]{1,0:T(2,128)} %bitcast.10, s32[2,8]{1,0:T(2,128)} %bitcast.11, f32[8,128]{1,0:T(8,128)} %broadcast_in_dim.12.freq, bf16[2,512,1024]{2,1,0:T(8,128)(2,1)} %bitcast.9, bf16[512,8192]{1,0:T(8,128)(2,1)} %bitcast.6), custom_call_target="tpu_custom_call" | custom-call | tf_op jit(solution)/shard_map/pallas_call | solution.py:671
  152.6 0.0 copy-start
  152.6 3.2 %copy.10 = bf16[1,1024,1024]{2,1,0:T(8,128)(2,1)} copy(bf16[1,1024,1024]{2,1,0:T(8,128)(2,1)} %bitcast.8) | data formatting | bytes 4194304
  155.8 0.0 copy-done
  155.8 1.3 copy.11
  (1 shorter events, 0.0 us)
Async XLA Ops:
  152.6 3.2 %copy-start = (bf16[512,2048]{1,0:T(8,128)(2,1)S(1)}, bf16[512,2048]{1,0:T(8,128)(2,1)}, u32[]{:S(2)}) copy-start(bf16[512,2048]{1,0:T(8,128)(2,1)} %get-tuple-element.5) | copy-start | bytes 6291460
